TPU v7x, 16 devices: a whole 2x2x2 slice. The times are simulated.
16 devices in a mesh: ep: 2 (over z), fsdp: 8 (over y, x, core).
Axes of the slice: x: 2, y: 2, z: 2, core: 2. Of those that a mesh axis runs over, the one named last changes fastest.
Arguments:
- x_in: bfloat16 [64, 512, 768], P(('ep', 'fsdp'))
- grad_y: bfloat16 [64, 512, 768], P(('ep', 'fsdp'))
- w_q: bfloat16 [768, 12, 64], P(('ep', 'fsdp'))
- w_k: bfloat16 [768, 12, 64], P(('ep', 'fsdp'))
- w_v: bfloat16 [768, 12, 64], P(('ep', 'fsdp'))
- w_o: bfloat16 [12, 64, 768], P(None, None, ('ep', 'fsdp'))
- gamma_attn: bfloat16 [768], P(('ep', 'fsdp'))
- gamma_mlp: bfloat16 [768], P(('ep', 'fsdp'))
- w_router: float32 [768, 8], P(('ep', 'fsdp'))
- w1_shared: bfloat16 [768, 3072], P(('ep', 'fsdp'))
- w3_shared: bfloat16 [768, 3072], P(('ep', 'fsdp'))
- w2_shared: bfloat16 [3072, 768], P(None, ('ep', 'fsdp'))
- w1_expert: bfloat16 [8, 768, 3072], P('ep', 'fsdp')
- w3_expert: bfloat16 [8, 768, 3072], P('ep', 'fsdp')
- w2_expert: bfloat16 [8, 3072, 768], P('ep', 'fsdp')
- expert_ids: int32 [64, 512], P(('ep', 'fsdp'))
Outputs:
- output 1: bfloat16 [64, 512, 768], P(('ep', 'fsdp'))
- output 2: bfloat16 [64, 512, 768], P(('ep', 'fsdp'))
- output 3: float32 [768, 12, 64], P(('ep', 'fsdp'))
- output 4: float32 [768, 12, 64], P(('ep', 'fsdp'))
- output 5: float32 [768, 12, 64], P(('ep', 'fsdp'))
- output 6: float32 [12, 64, 768], P(None, None, ('ep', 'fsdp'))
- output 7: float32 [768], P(('ep', 'fsdp'))
- output 8: float32 [768], P(('ep', 'fsdp'))
- output 9: float32 [768, 8], P(('ep', 'fsdp'))
- output 10: float32 [768, 3072], P(('ep', 'fsdp'))
- output 11: float32 [768, 3072], P(('ep', 'fsdp'))
- output 12: float32 [3072, 768], P(None, ('ep', 'fsdp'))
- output 13: float32 [8, 768, 3072], P('ep', 'fsdp')
- output 14: float32 [8, 768, 3072], P('ep', 'fsdp')
- output 15: float32 [8, 3072, 768], P('ep', 'fsdp')
All inputs are finite; a program needn't handle non-finite values.
Results may differ from a plain program's by a relative error of at most 0.02.
Values are sent between devices in bfloat16 or wider.
A program may use at most 1 GiB of HBM per device.

v0:
```python
import jax
import jax.numpy as jnp
from jax import lax
from jax.sharding import PartitionSpec as P

EPS_NORM = 1e-5
EPS_QK = 1e-6
ROPE_BASE = 500000.0
QUERY_BLOCK = 256
ALL_AXES = ('ep', 'fsdp')


def rms_norm(tokens, gamma_vec):
    tok_f32 = tokens.astype(jnp.float32)
    inv_rms = lax.rsqrt(jnp.mean(tok_f32 * tok_f32, axis=-1, keepdims=True) + EPS_NORM)
    return (tok_f32 * inv_rms * gamma_vec.astype(jnp.float32)).astype(jnp.bfloat16)


def swiglu_act(up_gate, up_lin):
    return (jax.nn.silu(up_gate) * up_lin).astype(jnp.bfloat16)


def rope_tables(seq_len, head_dim):
    half_dim = head_dim // 2
    inv_freq = ROPE_BASE ** (-(jnp.arange(half_dim, dtype=jnp.float32) * 2.0 / head_dim))
    angles = jnp.arange(seq_len, dtype=jnp.float32)[:, None] * inv_freq[None, :]
    return jnp.cos(angles), jnp.sin(angles)


def rope_norm(heads_in, cos_tab, sin_tab):
    half_dim = heads_in.shape[-1] // 2
    head_vals = heads_in.astype(jnp.float32)
    first_half = head_vals[..., :half_dim]
    second_half = head_vals[..., half_dim:]
    cos_b = cos_tab[:, None, :]
    sin_b = sin_tab[:, None, :]
    rotated = jnp.concatenate([first_half * cos_b - second_half * sin_b, second_half * cos_b + first_half * sin_b], axis=-1)
    rotated = rotated * lax.rsqrt(jnp.mean(rotated * rotated, axis=-1, keepdims=True) + EPS_QK)
    return rotated.astype(jnp.bfloat16)


def attention(q_proj, k_proj, v_proj):
    n_batch, seq_len, n_heads, head_dim = q_proj.shape
    kv_heads = k_proj.shape[2]
    q_per_kv = n_heads // kv_heads
    cos_tab, sin_tab = rope_tables(seq_len, head_dim)
    q_len = min(seq_len, QUERY_BLOCK)
    n_blocks = seq_len // q_len
    q_rot = rope_norm(q_proj, cos_tab, sin_tab).reshape(n_batch, n_blocks, q_len, kv_heads, q_per_kv, head_dim)
    q_blocks = jnp.moveaxis(q_rot, 1, 0)
    k_rot = rope_norm(k_proj, cos_tab, sin_tab)
    key_pos = jnp.arange(seq_len)

    def one_block(blk_args):
        q_blk, blk_start = blk_args
        scores = jnp.einsum('bqkgd,bskd->bkgqs', q_blk, k_rot, preferred_element_type=jnp.float32) * head_dim ** -0.5
        causal = (blk_start + jnp.arange(q_len))[:, None] >= key_pos[None, :]
        attn_probs = jax.nn.softmax(jnp.where(causal, scores, -1e30), axis=-1).astype(jnp.bfloat16)
        return jnp.einsum('bkgqs,bskd->bqkgd', attn_probs, v_proj, preferred_element_type=jnp.float32).astype(jnp.bfloat16)

    blocks_out = lax.map(jax.checkpoint(one_block), (q_blocks, jnp.arange(n_blocks) * q_len))
    return jnp.moveaxis(blocks_out, 0, 1).reshape(n_batch, seq_len, n_heads, head_dim)


def route_slots(flat_ids, n_experts, capacity):
    onehot = flat_ids[:, None] == jnp.arange(n_experts)[None, :]
    running = jnp.cumsum(onehot.astype(jnp.int32), axis=0)
    slot_idx = jnp.sum(jnp.where(onehot, running, 0), axis=1) - 1
    return onehot, flat_ids * capacity + slot_idx


def gather_one(w_block, axis_idx):
    return lax.all_gather(w_block, ALL_AXES, axis=axis_idx, tiled=True)


def gather_dense(w_q, w_k, w_v, w_o, gamma_attn, gamma_mlp, w_router, w1_shared, w3_shared, w2_shared):
    return (gather_one(w_q, 0), gather_one(w_k, 0), gather_one(w_v, 0), gather_one(w_o, 2), gather_one(gamma_attn, 0), gather_one(gamma_mlp, 0), gather_one(w_router, 0), gather_one(w1_shared, 0), gather_one(w3_shared, 0), gather_one(w2_shared, 1))


def gather_experts(w1_expert, w3_expert, w2_expert):
    return tuple(lax.all_gather(w_block, 'fsdp', axis=1, tiled=True) for w_block in (w1_expert, w3_expert, w2_expert))


def scatter_all(grad_full, axis_idx):
    return lax.psum_scatter(grad_full, ALL_AXES, scatter_dimension=axis_idx, tiled=True)


def scatter_experts(grad_full):
    return lax.psum_scatter(grad_full, 'fsdp', scatter_dimension=1, tiled=True)


def device_step(x_in, grad_y, w_q, w_k, w_v, w_o, gamma_attn, gamma_mlp, w_router, w1_shared, w3_shared, w2_shared, w1_expert, w3_expert, w2_expert, expert_ids):
    n_batch, seq_len, model_dim = x_in.shape
    n_tok = n_batch * seq_len
    n_heads, head_dim = w_q.shape[1], w_q.shape[2]
    n_experts = w_router.shape[1]
    e_local = w1_expert.shape[0]
    ep_size = n_experts // e_local
    capacity = 2 * n_tok // n_experts
    n_slots = n_experts * capacity
    wq_all, wk_all, wv_all, wo_all, ga_all, gm_all, wr_all, w1s_all, w3s_all, w2s_all = gather_dense(w_q, w_k, w_v, w_o, gamma_attn, gamma_mlp, w_router, w1_shared, w3_shared, w2_shared)
    w1e_all, w3e_all, w2e_all = gather_experts(w1_expert, w3_expert, w2_expert)

    tokens = x_in.reshape(n_tok, model_dim)
    normed1, norm1_pull = jax.vjp(rms_norm, tokens, ga_all.astype(jnp.float32))
    q_proj = jnp.einsum('td,dhk->thk', normed1, wq_all, preferred_element_type=jnp.float32).astype(jnp.bfloat16)
    k_proj = jnp.einsum('td,dhk->thk', normed1, wk_all, preferred_element_type=jnp.float32).astype(jnp.bfloat16)
    v_proj = jnp.einsum('td,dhk->thk', normed1, wv_all, preferred_element_type=jnp.float32).astype(jnp.bfloat16)
    attn_heads, attn_pull = jax.vjp(attention, q_proj.reshape(n_batch, seq_len, n_heads, head_dim), k_proj.reshape(n_batch, seq_len, -1, head_dim), v_proj.reshape(n_batch, seq_len, -1, head_dim))
    attn_flat = attn_heads.reshape(n_tok, n_heads, head_dim)
    attn_out = jnp.einsum('thk,hkd->td', attn_flat, wo_all, preferred_element_type=jnp.float32)
    hidden = (tokens.astype(jnp.float32) + attn_out).astype(jnp.bfloat16)
    normed2, norm2_pull = jax.vjp(rms_norm, hidden, gm_all.astype(jnp.float32))
    normed2_f = normed2.astype(jnp.float32)
    logits = jnp.dot(normed2, wr_all, preferred_element_type=jnp.float32, precision=lax.Precision.HIGHEST)
    onehot, dest_row = route_slots(expert_ids.reshape(n_tok), n_experts, capacity)
    gate_val = jax.nn.sigmoid(jnp.sum(jnp.where(onehot, logits, 0.0), axis=1))
    routed_in = (gate_val[:, None] * normed2_f).astype(jnp.bfloat16)
    send_rows = jnp.zeros((n_slots, model_dim), jnp.bfloat16).at[dest_row].set(routed_in)
    expert_rows = lax.all_to_all(send_rows.reshape(ep_size, e_local, capacity, model_dim), 'ep', 0, 0, tiled=True)
    up_gate = jnp.einsum('secd,edf->secf', expert_rows, w1e_all, preferred_element_type=jnp.float32)
    up_lin = jnp.einsum('secd,edf->secf', expert_rows, w3e_all, preferred_element_type=jnp.float32)
    act_routed, routed_pull = jax.vjp(swiglu_act, up_gate, up_lin)
    down_rows = jnp.einsum('secf,efd->secd', act_routed, w2e_all, preferred_element_type=jnp.float32).astype(jnp.bfloat16)
    back_rows = lax.all_to_all(down_rows, 'ep', 0, 0, tiled=True).reshape(n_slots, model_dim)
    routed = back_rows[dest_row]
    sh_gate = jnp.dot(normed2, w1s_all, preferred_element_type=jnp.float32)
    sh_lin = jnp.dot(normed2, w3s_all, preferred_element_type=jnp.float32)
    act_shared, shared_pull = jax.vjp(swiglu_act, sh_gate, sh_lin)
    shared_out = jnp.dot(act_shared, w2s_all, preferred_element_type=jnp.float32)
    layer_out = (hidden.astype(jnp.float32) + routed.astype(jnp.float32) + shared_out).astype(jnp.bfloat16)

    wq_all, wk_all, wv_all, wo_all, ga_all, gm_all, wr_all, w1s_all, w3s_all, w2s_all = gather_dense(w_q, w_k, w_v, w_o, gamma_attn, gamma_mlp, w_router, w1_shared, w3_shared, w2_shared)
    w1e_all, w3e_all, w2e_all = gather_experts(w1_expert, w3_expert, w2_expert)
    d_out = grad_y.reshape(n_tok, model_dim)
    d_act_shared = jnp.einsum('td,fd->tf', d_out, w2s_all, preferred_element_type=jnp.float32).astype(jnp.bfloat16)
    g_w2s = jnp.einsum('tf,td->fd', act_shared, d_out, preferred_element_type=jnp.float32)
    d_sh_gate, d_sh_lin = shared_pull(d_act_shared)
    d_sh_gate = d_sh_gate.astype(jnp.bfloat16)
    d_sh_lin = d_sh_lin.astype(jnp.bfloat16)
    d_normed2 = jnp.einsum('tf,df->td', d_sh_gate, w1s_all, preferred_element_type=jnp.float32) + jnp.einsum('tf,df->td', d_sh_lin, w3s_all, preferred_element_type=jnp.float32)
    g_w1s = jnp.einsum('td,tf->df', normed2, d_sh_gate, preferred_element_type=jnp.float32)
    g_w3s = jnp.einsum('td,tf->df', normed2, d_sh_lin, preferred_element_type=jnp.float32)

    d_send = jnp.zeros((n_slots, model_dim), jnp.bfloat16).at[dest_row].set(d_out)
    d_down = lax.all_to_all(d_send.reshape(ep_size, e_local, capacity, model_dim), 'ep', 0, 0, tiled=True)
    d_act_routed = jnp.einsum('secd,efd->secf', d_down, w2e_all, preferred_element_type=jnp.float32).astype(jnp.bfloat16)
    g_w2e = jnp.einsum('secf,secd->efd', act_routed, d_down, preferred_element_type=jnp.float32)
    d_up_gate, d_up_lin = routed_pull(d_act_routed)
    d_up_gate = d_up_gate.astype(jnp.bfloat16)
    d_up_lin = d_up_lin.astype(jnp.bfloat16)
    d_rows = (jnp.einsum('secf,edf->secd', d_up_gate, w1e_all, preferred_element_type=jnp.float32) + jnp.einsum('secf,edf->secd', d_up_lin, w3e_all, preferred_element_type=jnp.float32)).astype(jnp.bfloat16)
    g_w1e = jnp.einsum('secd,secf->edf', expert_rows, d_up_gate, preferred_element_type=jnp.float32)
    g_w3e = jnp.einsum('secd,secf->edf', expert_rows, d_up_lin, preferred_element_type=jnp.float32)
    d_back = lax.all_to_all(d_rows, 'ep', 0, 0, tiled=True).reshape(n_slots, model_dim)
    d_routed_in = d_back[dest_row].astype(jnp.float32)
    d_normed2 = d_normed2 + gate_val[:, None] * d_routed_in
    d_gate_val = jnp.sum(d_routed_in * normed2_f, axis=1) * gate_val * (1.0 - gate_val)
    d_logits = jnp.where(onehot, d_gate_val[:, None], 0.0)
    g_wr = jnp.einsum('td,te->de', normed2_f, d_logits, precision=lax.Precision.HIGHEST)
    d_normed2 = d_normed2 + jnp.einsum('te,de->td', d_logits, wr_all, precision=lax.Precision.HIGHEST)
    d_hid_norm, g_gm = norm2_pull(d_normed2.astype(jnp.bfloat16))
    d_hidden = (d_out.astype(jnp.float32) + d_hid_norm.astype(jnp.float32)).astype(jnp.bfloat16)

    d_attn = jnp.einsum('td,hkd->thk', d_hidden, wo_all, preferred_element_type=jnp.float32).astype(jnp.bfloat16)
    g_wo = jnp.einsum('thk,td->hkd', attn_flat, d_hidden, preferred_element_type=jnp.float32)
    d_q, d_k, d_v = attn_pull(d_attn.reshape(n_batch, seq_len, n_heads, head_dim))
    d_q = d_q.reshape(n_tok, n_heads, head_dim)
    d_k = d_k.reshape(n_tok, -1, head_dim)
    d_v = d_v.reshape(n_tok, -1, head_dim)
    g_wq = jnp.einsum('td,thk->dhk', normed1, d_q, preferred_element_type=jnp.float32)
    g_wk = jnp.einsum('td,thk->dhk', normed1, d_k, preferred_element_type=jnp.float32)
    g_wv = jnp.einsum('td,thk->dhk', normed1, d_v, preferred_element_type=jnp.float32)
    d_normed1 = jnp.einsum('thk,dhk->td', d_q, wq_all, preferred_element_type=jnp.float32) + jnp.einsum('thk,dhk->td', d_k, wk_all, preferred_element_type=jnp.float32) + jnp.einsum('thk,dhk->td', d_v, wv_all, preferred_element_type=jnp.float32)
    d_tok_norm, g_ga = norm1_pull(d_normed1.astype(jnp.bfloat16))
    d_x = (d_hidden.astype(jnp.float32) + d_tok_norm.astype(jnp.float32)).astype(jnp.bfloat16).reshape(n_batch, seq_len, model_dim)

    return (layer_out.reshape(n_batch, seq_len, model_dim), d_x, scatter_all(g_wq, 0), scatter_all(g_wk, 0), scatter_all(g_wv, 0), scatter_all(g_wo, 2), scatter_all(g_ga, 0), scatter_all(g_gm, 0), scatter_all(g_wr, 0), scatter_all(g_w1s, 0), scatter_all(g_w3s, 0), scatter_all(g_w2s, 1), scatter_experts(g_w1e), scatter_experts(g_w3e), scatter_experts(g_w2e))


def solution(mesh):
    tok_spec = P(ALL_AXES, None, None)
    mat_spec = P(ALL_AXES, None)
    vec_spec = P(ALL_AXES)
    wo_spec = P(None, None, ALL_AXES)
    w2s_spec = P(None, ALL_AXES)
    exp_spec = P('ep', 'fsdp', None)
    in_specs = (tok_spec, tok_spec, tok_spec, tok_spec, tok_spec, wo_spec, vec_spec, vec_spec, mat_spec, mat_spec, mat_spec, w2s_spec, exp_spec, exp_spec, exp_spec, mat_spec)
    out_specs = (tok_spec, tok_spec, tok_spec, tok_spec, tok_spec, wo_spec, vec_spec, vec_spec, mat_spec, mat_spec, mat_spec, w2s_spec, exp_spec, exp_spec, exp_spec)
    return jax.shard_map(device_step, mesh=mesh, in_specs=in_specs, out_specs=out_specs, check_vma=False)
```

profile of v0, /device:TPU:0, one launch (start us, length us, event | category | flops | bytes accessed | tf_op | source)
XLA Modules:
  0.0 2052.3 jit_solution(11828279034069612188)
XLA Ops:
  14.6 34.9 %all-reduce.9 = (bf16[768]{0:T(1024)(128)(2,1)S(1)}, bf16[768]{0:T(1024)(128)(2,1)S(1)}) all-reduce(bf16[768]{0:T(1024)(128)(2,1)S(1)} %dynamic-update-slice, bf16[768]{0:T(1024)(128)(2,1)S(1)} %dynamic-update-slice.1), channel_id=1, replica_groups=mesh['ep'=2,'fsdp'=8] {'ep','fsdp'}, use_global_device_ids=true, to_apply=%add.4 | all-reduce | flops 1536 | bytes 6144
  178.4 83.3 %while.31 = (s32[]{:T(128)}, bf16[2,4,256,12,1,64]{2,5,3,1,4,0:T(8,128)(2,1)}, s32[2]{0:T(128)S(1)}, bf16[2,4,256,12,1,64]{2,5,3,1,4,0:T(8,128)(2,1)}, bf16[4,51...) while((s32[]{:T(128)}, ...), condition=%wide.region_6.7_spmd.clone, body=%wide.region_3.6_spmd.clone.sunk | while | flops 1687003392 | bytes 123488440 | solution.py:61
  308.7 16.0 convolution_convert_fusion.2
  324.7 16.5 fusion.180
  341.2 38.3 %all-to-all-done = bf16[2,4,512,768]{3,2,1,0:T(8,128)(2,1)} async-done(((bf16[2,4,512,768]{3,2,1,0:T(8,128)(2,1)}), bf16[2,4,512,768]{3,2,1,0:T(8,128)(2,1)}, u32[]{:S(2)}, u32[]{:S(2)}) %all-to-all-start) | async-done | bytes 6291488 | tf_op jit(solution)/shard_map/all_to_all | solution.py:120
  386.1 32.4 %fusion.79 = f32[4,2,512,3072]{3,2,1,0:T(8,128)} fusion(bf16[4,768,3072]{2,1,0:T(8,128)(2,1)} %all-gather.22.cloned.1.call-done, bf16[2,4,512,768]{3,2,1,0:T(8,128)(2,1)} %all-to-all-done), kind=kOutput, calls=%fused_computation.99 | convolution fusion | flops 19327352832 | bytes 75497472 | tf_op jit(solution)/shard_map/secd,edf->secf/dot_general | solution.py:122
  418.6 37.5 %all-to-all-done.2 = bf16[2,4,512,768]{3,2,1,0:T(8,128)(2,1)} async-done(((bf16[2,4,512,768]{3,2,1,0:T(8,128)(2,1)}), bf16[2,4,512,768]{3,2,1,0:T(8,128)(2,1)}, u32[]{:S(2)}, u32[]{:S(2)}) %all-to-all-start.2) | async-done | bytes 6291488 | tf_op jit(solution)/shard_map/all_to_all | solution.py:146
  456.1 27.4 %convolution_convert_fusion.1 = bf16[4,2,512,3072]{3,2,1,0:T(8,128)(2,1)} fusion(bf16[4,3072,768]{2,1,0:T(8,128)(2,1)} %all-gather.24.cloned.1.call-done, bf16[2,4,512,768]{3,2,1,0:T(8,128)(2,1)} %all-to-all-done.2), kind=kOutput, calls=%fused_computation.96 | convolution fusion | flops 19339935744 | bytes 50331648 | tf_op jit(solution)/shard_map/secd,efd->secf/dot_general | solution.py:147
  483.5 23.9 %all-gather.20.cloned.1.call-done = bf16[4,768,3072]{2,1,0:T(8,128)(2,1)} async-done(((bf16[4,96,3072]{2,1,0:T(8,128)(2,1)}), bf16[4,768,3072]{2,1,0:T(8,128)(2,1)}) %all-gather.20.cloned.1.call-update) | async-done | bytes 18874384 | tf_op jit(solution)/shard_map/all_gather | solution.py:81
  507.4 69.7 %fusion.62 = (bf16[2,4,512,3072]{3,2,0,1:T(8,128)(2,1)}, bf16[2,4,512,3072]{3,2,0,1:T(8,128)(2,1)}, bf16[2,4,512,3072]{3,2,0,1:T(8,128)(2,1)}) fusion(f32[4,2,512,3072]{3,2,1,0:T(8,128)} %fusion.79, bf16[4,2,512,3072]{3,2,1,0:T(8,128)(2,1)} %convolution_convert_fusion.1, bf16[4,768,3072]{2,1,0:T(8,128)(2,1)} %all-gather.20.cloned.1.call-done, ...), kind=kOutput, calls=%fused_computation.70 | convolution fusion | flops 19541262336 | bytes 176160768 | tf_op jit(solution)/shard_map/secd,edf->secf/dot_general | solution.py:121
  577.1 29.3 %fusion.77 = f32[4,2,512,768]{3,2,1,0:T(8,128)} fusion(bf16[2,4,512,3072]{3,2,0,1:T(8,128)(2,1)} %get-tuple-element.457, bf16[4,768,3072]{2,1,0:T(8,128)(2,1)} %all-gather.22.cloned.1.call-done), kind=kOutput, calls=%fused_computation.97 | convolution fusion | flops 19327352832 | bytes 56623104 | tf_op jit(solution)/shard_map/secf,edf->secd/dot_general | solution.py:152
  606.4 29.7 %fusion.114 = bf16[2,4,512,768]{3,2,0,1:T(8,128)(2,1)} fusion(f32[4,2,512,768]{3,2,1,0:T(8,128)} %fusion.77, bf16[2,4,512,3072]{3,2,0,1:T(8,128)(2,1)} %get-tuple-element.455, bf16[4,768,3072]{2,1,0:T(8,128)(2,1)} %all-gather.20.cloned.1.call-done), kind=kOutput, calls=%fused_computation.151 | convolution fusion | flops 19333644288 | bytes 62914560 | tf_op jit(solution)/shard_map/secf,edf->secd/dot_general | solution.py:152
  648.7 34.0 %fusion.71 = (bf16[2048,3072]{1,0:T(8,128)(2,1)}, bf16[2048,3072]{1,0:T(8,128)(2,1)}, bf16[2048,3072]{1,0:T(8,128)(2,1)}) fusion(f32[2048,3072]{1,0:T(8,128)} %fusion.180, bf16[2048,3072]{1,0:T(8,128)(2,1)} %convolution_convert_fusion.2, bf16[768,3072]{1,0:T(8,128)(2,1)} %all-gather.26.cloned.1.call-done, bf16[2048,768]{1,0:T(8,128)(2,1)S(1)} %copy-done.8, ...), kind=kOutput, calls=%fused_computation.88 | convolution fusion | flops 9776922624 | bytes 83373056 | tf_op jit(solution)/shard_map/dot_general | solution.py:127
  682.7 36.3 %all-to-all-done.3 = bf16[2,4,512,768]{3,2,1,0:T(8,128)(2,1)} async-done(((bf16[2,4,512,768]{3,2,1,0:T(8,128)(2,1)}), bf16[2,4,512,768]{3,2,1,0:T(8,128)(2,1)}, u32[]{:S(2)}, u32[]{:S(2)}) %all-to-all-start.3) | async-done | bytes 6291488 | tf_op jit(solution)/shard_map/all_to_all | solution.py:155
  772.0 16.2 fusion.192
  845.0 200.5 %while.32 = (s32[]{:T(128)}, bf16[4,512,12,64]{1,3,2,0:T(8,128)(2,1)}, bf16[4,512,12,64]{1,3,2,0:T(8,128)(2,1)}, bf16[2,4,256,12,1,64]{2,5,3,1,4,0:T(8,128)(2,1)...) while((s32[]{:T(128)}, ...), condition=%wide.region_20.21_spmd.clone, body=%wide.region_16.20_spmd.clone.sunk | while | flops 4275962112 | bytes 314857920 | solution.py:61
  872.1 18.3 fusion.265
  890.4 19.5 bitcast_add_fusion.7
  923.3 19.9 bitcast_dynamic-update-slice_fusion.5
  972.0 19.5 fusion.265
  991.5 18.8 bitcast_add_fusion.7
  1024.0 19.6 bitcast_dynamic-update-slice_fusion.5
  1126.7 31.4 %fusion.88 = f32[4,768,3072]{2,1,0:T(8,128)} fusion(bf16[2,4,512,768]{3,2,1,0:T(8,128)(2,1)} %all-to-all-done, bf16[2,4,512,3072]{3,2,0,1:T(8,128)(2,1)} %get-tuple-element.455), kind=kOutput, calls=%fused_computation.108 | convolution fusion | flops 19327352832 | bytes 69206016 | tf_op jit(solution)/shard_map/secd,secf->edf/dot_general | solution.py:153
  1158.1 31.0 %fusion.91 = f32[4,768,3072]{2,1,0:T(8,128)} fusion(bf16[2,4,512,768]{3,2,1,0:T(8,128)(2,1)} %all-to-all-done, bf16[2,4,512,3072]{3,2,0,1:T(8,128)(2,1)} %get-tuple-element.457), kind=kOutput, calls=%fused_computation.109 | convolution fusion | flops 19327352832 | bytes 69206016 | tf_op jit(solution)/shard_map/secd,secf->edf/dot_general | solution.py:154
  1189.1 31.3 %convolution_bitcast_fusion = f32[4,3072,768]{2,1,0:T(8,128)} fusion(bf16[2,4,512,3072]{3,2,0,1:T(8,128)(2,1)} %get-tuple-element.456, bf16[2,4,512,768]{3,2,1,0:T(8,128)(2,1)} %all-to-all-done.2), kind=kOutput, calls=%fused_computation.110 | convolution fusion | flops 19327352832 | bytes 69206016 | tf_op jit(solution)/shard_map/secf,secd->efd/dot_general | solution.py:148
  1220.5 28.5 %convert_bitcast_fusion.1 = bf16[2,4,512,768]{3,2,0,1:T(8,128)(2,1)S(1)} fusion(bf16[2,4,512,3072]{3,2,0,1:T(8,128)(2,1)} %get-tuple-element.456, bf16[4,3072,768]{2,1,0:T(8,128)(2,1)} %all-gather.24.cloned.1.call-done), kind=kOutput, calls=%fused_computation.174 | convolution fusion | flops 19330498560 | bytes 50331648 | tf_op jit(solution)/shard_map/secf,efd->secd/dot_general | solution.py:124
  1258.5 86.4 %all-to-all-done.1 = bf16[2,4,512,768]{3,2,1,0:T(8,128)(2,1)} async-done(((bf16[2,4,512,768]{3,2,1,0:T(8,128)(2,1)}), bf16[2,4,512,768]{3,2,1,0:T(8,128)(2,1)}, u32[]{:S(2)}, u32[]{:S(2)}) %all-to-all-start.1) | async-done | bytes 6291488 | tf_op jit(solution)/shard_map/all_to_all | solution.py:125
  1391.4 32.5 %all-reduce.8 = (f32[768]{0:T(1024)S(1)}, f32[768]{0:T(1024)S(1)}) all-reduce(f32[768]{0:T(1024)S(1)} %get-tuple-element.411, f32[768]{0:T(1024)S(1)} %copy-done.77), channel_id=6, replica_groups=mesh['ep'=2,'fsdp'=8] {'ep','fsdp'}, use_global_device_ids=true, to_apply=%region_29.30.clone | all-reduce | flops 1536 | bytes 12288
  1431.6 16.3 fusion.112
  1449.4 147.5 %reduce-scatter.28.cloned.1.call-done = f32[4,96,3072]{2,1,0:T(8,128)} async-done(((f32[4,768,3072]{2,1,0:T(8,128)}), f32[4,96,3072]{2,1,0:T(8,128)}) %reduce-scatter.28.cloned.1.call-update) | async-done | bytes 4718608 | tf_op jit(solution)/shard_map/reduce_scatter | solution.py:89
  1596.9 224.1 %reduce-scatter.30.cloned.1.call-done = f32[4,96,3072]{2,1,0:T(8,128)} async-done(((f32[4,768,3072]{2,1,0:T(8,128)}), f32[4,96,3072]{2,1,0:T(8,128)}) %reduce-scatter.30.cloned.1.call-update) | async-done | bytes 4718608 | tf_op jit(solution)/shard_map/reduce_scatter | solution.py:89
  1821.0 224.2 %reduce-scatter.32.cloned.1.call-done = f32[4,384,768]{2,1,0:T(8,128)} async-done(((f32[4,3072,768]{2,1,0:T(8,128)}), f32[4,384,768]{2,1,0:T(8,128)}) %reduce-scatter.32.cloned.1.call-update) | async-done | bytes 4718608 | tf_op jit(solution)/shard_map/reduce_scatter | solution.py:89
  (410 shorter events, 624.7 us)
Async XLA Ops:
  7.2 42.2 %copy-start.10 = (bf16[4,512,768]{2,1,0:T(8,128)(2,1)S(1)}, bf16[4,512,768]{2,1,0:T(8,128)(2,1)}, u32[]{:S(2)}) copy-start(bf16[4,512,768]{2,1,0:T(8,128)(2,1)} %param.20) | copy-start | bytes 9437188
  7.2 47.6 %copy-start.79 = (f32[48,8]{0,1:T(8,128)S(1)}, f32[48,8]{0,1:T(8,128)}, u32[]{:S(2)}) copy-start(f32[48,8]{0,1:T(8,128)} %param.28) | copy-start | bytes 4612
  7.2 79.4 %all-gather.14.cloned.1.call-start = ((), (), s32[]{:S(2)}) async-start(), calls=%async_computation.16 | async-start | bytes 2506752 | tf_op jit(solution)/shard_map/all_gather | solution.py:73
  8.0 100.8 %all-gather.12.cloned.1.call-start = ((), (), s32[]{:S(2)}) async-start(), calls=%async_computation.15 | async-start | bytes 2506752 | tf_op jit(solution)/shard_map/all_gather | solution.py:73
  8.7 151.4 %all-gather.16.cloned.1.call-start = ((), (), s32[]{:S(2)}) async-start(), calls=%async_computation.17 | async-start | bytes 2506752 | tf_op jit(solution)/shard_map/all_gather | solution.py:73
  9.5 266.4 %all-gather.18.cloned.1.call-start = ((), (), s32[]{:S(2)}) async-start(), calls=%async_computation.18 | async-start | bytes 2506752 | tf_op jit(solution)/shard_map/all_gather | solution.py:73
  10.0 298.7 %all-gather.30.cloned.1.call-start = ((), (), s32[]{:S(2)}) async-start(), calls=%async_computation.24 | async-start | bytes 5013504 | tf_op jit(solution)/shard_map/all_gather | solution.py:73
  10.6 314.1 %all-gather.28.cloned.1.call-start = ((), (), s32[]{:S(2)}) async-start(), calls=%async_computation.23 | async-start | bytes 5013504 | tf_op jit(solution)/shard_map/all_gather | solution.py:73
  11.2 374.9 %all-gather.22.cloned.1.call-start = ((), (), s32[]{:S(2)}) async-start(), calls=%async_computation.20 | async-start | bytes 21233664 | tf_op jit(solution)/shard_map/all_gather | solution.py:81
  11.9 444.2 %all-gather.24.cloned.1.call-start = ((), (), s32[]{:S(2)}) async-start(), calls=%async_computation.21 | async-start | bytes 21233664 | tf_op jit(solution)/shard_map/all_gather | solution.py:81
  12.7 494.7 %all-gather.20.cloned.1.call-start = ((), (), s32[]{:S(2)}) async-start(), calls=%async_computation.19 | async-start | bytes 21233664 | tf_op jit(solution)/shard_map/all_gather | solution.py:81
  13.4 635.2 %all-gather.26.cloned.1.call-start = ((), (), s32[]{:S(2)}) async-start(), calls=%async_computation.22 | async-start | bytes 5013504 | tf_op jit(solution)/shard_map/all_gather | solution.py:73
  51.1 76.5 %copy-start.47 = (f32[512,32]{0,1:T(8,128)}, f32[512,32]{0,1:T(8,128)S(1)}, u32[]{:S(2)}) copy-start(f32[512,32]{0,1:T(8,128)S(1)} %get-tuple-element.479) | copy-start | bytes 196612
  51.1 76.5 %copy-start.49 = (f32[512,32]{0,1:T(8,128)}, f32[512,32]{0,1:T(8,128)S(1)}, u32[]{:S(2)}) copy-start(f32[512,32]{0,1:T(8,128)S(1)} %get-tuple-element.480) | copy-start | bytes 196612
  302.4 77.2 %all-to-all-start = ((bf16[2,4,512,768]{3,2,1,0:T(8,128)(2,1)}), bf16[2,4,512,768]{3,2,1,0:T(8,128)(2,1)}, u32[]{:S(2)}, u32[]{:S(2)}) async-start(bf16[2,4,512,768]{3,2,1,0:T(8,128)(2,1)} %bitcast.472), calls=%async_computation | async-start | bytes 12582912 | tf_op jit(solution)/shard_map/all_to_all | solution.py:120
  379.6 76.5 %all-to-all-start.2 = ((bf16[2,4,512,768]{3,2,1,0:T(8,128)(2,1)}), bf16[2,4,512,768]{3,2,1,0:T(8,128)(2,1)}, u32[]{:S(2)}, u32[]{:S(2)}) async-start(bf16[2,4,512,768]{3,2,1,0:T(8,128)(2,1)} %bitcast.471), calls=%async_computation.2 | async-start | bytes 12582912 | tf_op jit(solution)/shard_map/all_to_all | solution.py:146
  642.0 77.1 %all-to-all-start.3 = ((bf16[2,4,512,768]{3,2,1,0:T(8,128)(2,1)}), bf16[2,4,512,768]{3,2,1,0:T(8,128)(2,1)}, u32[]{:S(2)}, u32[]{:S(2)}) async-start(bf16[2,4,512,768]{3,2,1,0:T(8,128)(2,1)} %copy.145), calls=%async_computation.3 | async-start | bytes 12582912 | tf_op jit(solution)/shard_map/all_to_all | solution.py:155
  648.6 70.5 %copy-start.67 = (s32[2048]{0:T(1024)S(1)}, s32[2048]{0:T(1024)}, u32[]{:S(2)}) copy-start(s32[2048]{0:T(1024)} %broadcast_clamp_fusion) | copy-start | bytes 24580
  648.6 799.3 %reduce-scatter.34.cloned.1.call-start = ((), (), s32[]{:S(2)}) async-start(), calls=%async_computation.35 | async-start | bytes 417792
  740.5 708.8 %reduce-scatter.22.cloned.1.call-start = ((), (), s32[]{:S(2)}) async-start(), calls=%async_computation.29 | async-start | bytes 10027008 | tf_op jit(solution)/shard_map/reduce_scatter | solution.py:85
  756.3 693.1 %reduce-scatter.24.cloned.1.call-start = ((), (), s32[]{:S(2)}) async-start(), calls=%async_computation.30 | async-start | bytes 10027008 | tf_op jit(solution)/shard_map/reduce_scatter | solution.py:85
  771.9 677.4 %reduce-scatter.26.cloned.1.call-start = ((), (), s32[]{:S(2)}) async-start(), calls=%async_computation.31 | async-start | bytes 10027008 | tf_op jit(solution)/shard_map/reduce_scatter | solution.py:85
  788.2 661.1 %reduce-scatter.14.cloned.1.call-start = ((), (), s32[]{:S(2)}) async-start(), calls=%async_computation.25 | async-start | bytes 5013504 | tf_op jit(solution)/shard_map/reduce_scatter | solution.py:85
  1098.6 350.8 %reduce-scatter.16.cloned.1.call-start = ((), (), s32[]{:S(2)}) async-start(), calls=%async_computation.26 | async-start | bytes 5013504 | tf_op jit(solution)/shard_map/reduce_scatter | solution.py:85
  1108.0 341.4 %reduce-scatter.18.cloned.1.call-start = ((), (), s32[]{:S(2)}) async-start(), calls=%async_computation.27 | async-start | bytes 5013504 | tf_op jit(solution)/shard_map/reduce_scatter | solution.py:85
  1117.0 332.4 %reduce-scatter.20.cloned.1.call-start = ((), (), s32[]{:S(2)}) async-start(), calls=%async_computation.28 | async-start | bytes 5013504 | tf_op jit(solution)/shard_map/reduce_scatter | solution.py:85
  1126.6 470.3 %reduce-scatter.28.cloned.1.call-start = ((), (), s32[]{:S(2)}) async-start(), calls=%async_computation.32 | async-start | bytes 42467328 | tf_op jit(solution)/shard_map/reduce_scatter | solution.py:89
  1158.1 663.0 %reduce-scatter.30.cloned.1.call-start = ((), (), s32[]{:S(2)}) async-start(), calls=%async_computation.33 | async-start | bytes 42467328 | tf_op jit(solution)/shard_map/reduce_scatter | solution.py:89
  1189.1 856.2 %reduce-scatter.32.cloned.1.call-start = ((), (), s32[]{:S(2)}) async-start(), calls=%async_computation.34 | async-start | bytes 42467328 | tf_op jit(solution)/shard_map/reduce_scatter | solution.py:89
  1252.1 92.8 %copy-start.68 = (s32[2048]{0:T(1024)S(1)}, s32[2048]{0:T(1024)}, u32[]{:S(2)}) copy-start(s32[2048]{0:T(1024)} %broadcast_clamp_fusion) | copy-start | bytes 24580
  1252.1 92.8 %all-to-all-start.1 = ((bf16[2,4,512,768]{3,2,1,0:T(8,128)(2,1)}), bf16[2,4,512,768]{3,2,1,0:T(8,128)(2,1)}, u32[]{:S(2)}, u32[]{:S(2)}) async-start(bf16[2,4,512,768]{3,2,1,0:T(8,128)(2,1)} %copy.143), calls=%async_computation.1 | async-start | bytes 12582912 | tf_op jit(solution)/shard_map/all_to_all | solution.py:125
  1381.0 44.0 %copy-start.63 = (f32[1,4,4,128]{3,1,2,0:T(4,128)S(1)}, f32[1,4,4,128]{3,1,2,0:T(4,128)}, u32[]{:S(2)}) copy-start(f32[1,4,4,128]{3,1,2,0:T(4,128)} %copy-done.62) | copy-start | bytes 24580
  (96 other events, 906.3 us)
Sparse Core Ops, SparseCore 0:
  10.3 32.8 all-gather.13
  45.4 29.8 all-gather.11
  77.5 29.6 all-gather.15
  109.3 29.6 all-gather.17
  141.0 36.9 all-gather.29
  180.1 37.0 all-gather.27
  219.0 94.8 all-gather.21
  315.8 94.8 all-gather.23
  412.5 94.8 all-gather.19
  509.5 36.9 all-gather.25
  740.7 46.2 reduce-scatter.33
  792.1 80.0 reduce-scatter.21
  877.4 80.0 reduce-scatter.23
  962.6 80.1 reduce-scatter.25
  1098.7 60.8 reduce-scatter.13
  1164.4 60.6 reduce-scatter.15
  1229.9 75.4 reduce-scatter.17
  1310.1 62.4 reduce-scatter.19
  1376.8 220.0 reduce-scatter.27
  1600.9 220.0 reduce-scatter.29
  1825.2 220.0 reduce-scatter.31
where the time goes:
time: 2060 us; the launch traced here: 2050 us
  waiting for transfers between devices  825 us (40%)
  matrix products  792 us (38%)
  local copies, waits for them, and re-layouts  183 us (9%)
  other arithmetic  129 us (6%)
  blocking collectives  80.2 us (4%)
  starting transfers between devices  26.7 us (1%)
    reduce_scatter x3, waiting for transfers between devices, scatter_experts(): return lax.psum_scatter(grad_full, 'fsdp', scatter_dimension=1, tiled=True)  596 us
    dot_general x8, matrix products, one_block(): jnp.einsum('bqkgd,bskd->bkgqs', q_blk, k_rot, preferred_element_type=jnp....  126 us
    dot_general x6, matrix products, one_block(): jnp.einsum('bkgqs,bskd->bqkgd', attn_probs, v_proj, preferred_element_typ...  90.9 us
    all_to_all x1, waiting for transfers between devices, device_step(): lax.all_to_all(down_rows, 'ep', 0, 0, tiled=True)  86.4 us
    dot_general x1, matrix products, device_step(): jnp.einsum('secd,edf->secf', expert_rows, w1e_all, preferred_element_type...  69.7 us
    unnamed x2, blocking collectives  67.4 us
    reduce_sum x4, other arithmetic, one_block(): jax.nn.softmax(jnp.where(causal, scores, -1e+30), axis=-1)  49.2 us
  transfers between devices with their start and end apart: 25, of which 8 were waited for; matrix products, arithmetic and copies ran while one was open for 52% of the time, Pallas kernels for 0%

commit v1 on v0

v1 whole, which is shorter than its diff:
```python
import functools
import math

import jax
import jax.numpy as jnp
from jax import lax
from jax.experimental import pallas as pl
from jax.experimental.pallas import tpu as pltpu
from jax.sharding import PartitionSpec as P


EPS_NORM = 1e-5
EPS_QK = 1e-6
ROPE_BASE = 500000.0
ALL_AXES = ('ep', 'fsdp')
PAIRS = [[0, 1], [2, 3], [4, 5], [6, 7]]
BF = jnp.bfloat16
F32 = jnp.float32
HEAD = 64
LANES = 128
Q_BLOCK = 256


def dot_nn(a, b):
    return lax.dot_general(a, b, (((1,), (0,)), ((), ())), preferred_element_type=F32)


def dot_nt(a, b):
    return lax.dot_general(a, b, (((1,), (1,)), ((), ())), preferred_element_type=F32)


def cost(flops, nbytes, trans=0):
    return pl.CostEstimate(flops=int(flops), bytes_accessed=int(nbytes), transcendentals=int(trans))


def params(*sem):
    return pltpu.CompilerParams(dimension_semantics=sem)


def head_tables(seq_len):
    half = HEAD // 2
    inv_freq = ROPE_BASE ** (-(jnp.arange(half, dtype=F32) * 2.0 / HEAD))
    angles = jnp.arange(seq_len, dtype=F32)[:, None] * inv_freq[None, :]
    cos, sin = jnp.cos(angles), jnp.sin(angles)
    cos_t = jnp.concatenate([cos, cos, cos, cos], axis=1)
    sin_t = jnp.concatenate([-sin, sin, -sin, sin], axis=1)
    return cos_t, sin_t


def swap_halves(x, low):
    return jnp.where(low, pltpu.roll(x, LANES - HEAD // 2, 1), pltpu.roll(x, HEAD // 2, 1))


def head_sum(x, first):
    a = jnp.sum(jnp.where(first, x, 0.0), axis=1, keepdims=True)
    b = jnp.sum(jnp.where(first, 0.0, x), axis=1, keepdims=True)
    return jnp.where(first, a, b)


def rope_unit(x, cos_t, sin_t, first, low):
    x = x.astype(F32)
    rot = x * cos_t + swap_halves(x, low) * sin_t
    inv = lax.rsqrt(head_sum(rot * rot, first) * (1.0 / HEAD) + EPS_QK)
    return rot, inv


def lane_masks(rows):
    lane = lax.broadcasted_iota(jnp.int32, (rows, LANES), 1)
    return lane < HEAD, (lane & (HEAD - 1)) < HEAD // 2


def causal_probs(k_rot, q_head, n_keys):
    scores = dot_nt(k_rot, q_head)
    e = jnp.exp2(scores * (HEAD ** -0.5 * math.log2(math.e)))
    n_q = q_head.shape[0]
    row = lax.broadcasted_iota(jnp.int32, (n_q, n_q), 0)
    col = lax.broadcasted_iota(jnp.int32, (n_q, n_q), 1)
    tail = jnp.where(row <= col, e[n_keys - n_q:], 0.0)
    e = tail if n_keys == n_q else jnp.concatenate([e[:n_keys - n_q], tail], axis=0)
    return e, 1.0 / jnp.sum(e, axis=0, keepdims=True)


def attn_fwd_kernel(q_ref, k_ref, v_ref, cos_ref, sin_ref, *rest):
    o_ref = rest[-1]
    seq = q_ref.shape[0]
    first, low = lane_masks(seq)
    cos_t, sin_t = cos_ref[...], sin_ref[...]
    q_rot, q_inv = rope_unit(q_ref[...], cos_t, sin_t, first, low)
    k_rot, k_inv = rope_unit(k_ref[...], cos_t, sin_t, first, low)
    q_unit = q_rot * q_inv
    k_unit = (k_rot * k_inv).astype(BF)
    v_t = v_ref[...].astype(F32).T.astype(BF)
    heads = [jnp.where(first, q_unit, 0.0).astype(BF), jnp.where(first, 0.0, q_unit).astype(BF)]
    for j in range(seq // Q_BLOCK):
        n_keys = (j + 1) * Q_BLOCK
        rows = slice(j * Q_BLOCK, n_keys)
        parts = []
        for h in range(2):
            e, inv_sum = causal_probs(k_unit[:n_keys], heads[h][rows], n_keys)
            probs = (e * inv_sum).astype(BF)
            out_t = dot_nn(v_t[:, :n_keys], probs)
            parts.append(out_t[h * HEAD:(h + 1) * HEAD])
        o_ref[rows, :] = jnp.concatenate(parts, axis=0).T.astype(BF)


def attn_bwd_kernel(q_ref, k_ref, v_ref, do_ref, cos_ref, sin_ref, *rest):
    dq_ref, dk_ref, dv_ref, dk_acc, dv_acc = rest[-5:]
    seq = q_ref.shape[0]
    first, low = lane_masks(seq)
    cos_t, sin_t = cos_ref[...], sin_ref[...]
    q_rot, q_inv = rope_unit(q_ref[...], cos_t, sin_t, first, low)
    k_rot, k_inv = rope_unit(k_ref[...], cos_t, sin_t, first, low)
    q_unit = q_rot * q_inv
    k_f32 = k_rot * k_inv
    k_unit = k_f32.astype(BF)
    k_t = k_f32.T.astype(BF)
    v = v_ref[...]
    d_out = do_ref[...].astype(F32)
    q_heads = [jnp.where(first, q_unit, 0.0).astype(BF), jnp.where(first, 0.0, q_unit).astype(BF)]
    do_heads = [jnp.where(first, d_out, 0.0).astype(BF), jnp.where(first, 0.0, d_out).astype(BF)]

    def unrope(d_unit, rot, inv, first, low, cos_t, sin_t):
        t = head_sum(d_unit * rot, first) * (1.0 / HEAD)
        d_rot = inv * d_unit - rot * (inv * inv * inv * t)
        return (d_rot * cos_t - swap_halves(d_rot, low) * sin_t).astype(BF)

    dk_acc[...] = jnp.zeros_like(dk_acc)
    dv_acc[...] = jnp.zeros_like(dv_acc)
    for j in range(seq // Q_BLOCK):
        n_keys = (j + 1) * Q_BLOCK
        rows = slice(j * Q_BLOCK, n_keys)
        parts = []
        for h in range(2):
            qh, doh = q_heads[h][rows], do_heads[h][rows]
            e, inv_sum = causal_probs(k_unit[:n_keys], qh, n_keys)
            probs = e * inv_sum
            d_probs = dot_nt(v[:n_keys], doh)
            delta = jnp.sum(probs * d_probs, axis=0, keepdims=True)
            d_scores = (probs * (d_probs - delta) * HEAD ** -0.5).astype(BF)
            dv_acc[:n_keys, :] += dot_nn(probs.astype(BF), doh)
            dk_acc[:n_keys, :] += dot_nn(d_scores, qh)
            dq_t = dot_nn(k_t[:, :n_keys], d_scores)
            parts.append(dq_t[h * HEAD:(h + 1) * HEAD])
        d_unit = jnp.concatenate(parts, axis=0).T
        dq_ref[rows, :] = unrope(d_unit, q_rot[rows], q_inv[rows], first[rows], low[rows], cos_t[rows], sin_t[rows])
    dk_ref[...] = unrope(dk_acc[...], k_rot, k_inv, first, low, cos_t, sin_t)
    dv_ref[...] = dv_acc[...].astype(BF)


def attn_call(kernel, arrays, offsets, tables, outs, n_out, lo, hi, seq, width, scratch, flops):
    n_tok = arrays[0].shape[0]
    groups = width // LANES
    block = lambda off: pl.BlockSpec((seq, LANES), lambda b, g: (b + lo, g + off))
    table = pl.BlockSpec((seq, LANES), lambda b, g: (0, 0))
    n_in = len(arrays) + 2
    rows = (hi - lo) * seq
    return pl.pallas_call(
        kernel,
        grid=(hi - lo, groups),
        in_specs=[block(off) for off in offsets] + [table, table] + [pl.BlockSpec(memory_space=pl.ANY)] * len(outs),
        out_specs=[block(0)] * n_out,
        out_shape=[jax.ShapeDtypeStruct((n_tok, width), BF)] * n_out,
        scratch_shapes=scratch,
        input_output_aliases={n_in + i: i for i in range(len(outs))},
        compiler_params=params('arbitrary', 'arbitrary'),
        cost_estimate=cost(flops * rows * seq * width, 2 * (len(arrays) + n_out) * rows * width),
    )(*arrays, *tables, *outs)


def attn_fwd(qkv, tables, seq, outs, lo, hi):
    width = qkv.shape[1] // 3
    groups = width // LANES
    return attn_call(attn_fwd_kernel, [qkv] * 3, [0, groups, 2 * groups], tables, outs, 1, lo, hi, seq, width, [], 20)


def attn_bwd(qkv, d_out, tables, seq, outs, lo, hi):
    width = d_out.shape[1]
    groups = width // LANES
    scratch = [pltpu.VMEM((seq, LANES), F32)] * 2
    return attn_call(attn_bwd_kernel, [qkv] * 3 + [d_out], [0, groups, 2 * groups, 0], tables, outs, 3, lo, hi, seq, width, scratch, 50)


def join_halves(ref, out):
    _, n, rows, _ = ref.shape
    for s in range(n):
        for h in range(2):
            lo = (2 * s + h) * rows
            out[lo:lo + rows, :] = ref[h, s]


def swiglu_kernel(chunk, split, x_ref, dy_ref, w1_ref, w3_ref, w2_ref, act_ref, dg_ref, dl_ref, *joined):
    if split:
        @pl.when(pl.program_id(1) == 0)
        def _():
            for ref, out in zip((w1_ref, w3_ref, w2_ref), joined):
                join_halves(ref, out)

        w1_ref, w3_ref, w2_ref = joined
    down = dot_nt if split else dot_nn
    for c in range(x_ref.shape[0] // chunk):
        rows = slice(c * chunk, (c + 1) * chunk)
        x = x_ref[rows, :]
        gate = dot_nn(x, w1_ref[...])
        lin = dot_nn(x, w3_ref[...])
        d_act = down(dy_ref[rows, :], w2_ref[...]).astype(BF).astype(F32)
        sig = jax.nn.sigmoid(gate)
        silu = gate * sig
        act_ref[rows, :] = (silu * lin).astype(BF)
        dl_ref[rows, :] = (d_act * silu).astype(BF)
        dg_ref[rows, :] = (d_act * lin * (sig * (1.0 + gate * (1.0 - sig)))).astype(BF)


def swiglu(x, d_y, weights, width, split, tm=1024, fb=768, chunk=1024):
    n_tok, dim = x.shape
    tok = pl.BlockSpec((tm, dim), lambda f, t: (t, 0))
    if split:
        up = [pl.BlockSpec(w.shape[:3] + (fb,), lambda f, t: (0, 0, 0, f)) for w in weights[:2]]
        part = weights[2].shape[2]
        w_specs = up + [pl.BlockSpec((2, fb // (2 * part), part, dim), lambda f, t: (0, f, 0, 0))]
    else:
        w_specs = [pl.BlockSpec((dim, fb), lambda f, t, off=i * width // fb: (0, f + off)) for i in range(3)]
        weights = [weights] * 3
    out = pl.BlockSpec((tm, fb), lambda f, t: (t, f))
    return pl.pallas_call(
        functools.partial(swiglu_kernel, chunk, split),
        grid=(width // fb, n_tok // tm),
        in_specs=[tok, tok] + w_specs,
        out_specs=[out] * 3,
        out_shape=[jax.ShapeDtypeStruct((n_tok, width), BF)] * 3,
        scratch_shapes=[pltpu.VMEM((dim, fb), BF)] * 2 + [pltpu.VMEM((fb, dim), BF)] if split else [],
        compiler_params=params('arbitrary', 'arbitrary'),
        cost_estimate=cost(6 * n_tok * dim * width, 6 * n_tok * width + 8 * n_tok * dim + 6 * dim * width, 2 * n_tok * width),
    )(x, d_y, *weights)


def mm_kernel(modes, n_extra, combine, split, *refs):
    n = len(modes)
    out = refs[2 * n + n_extra]
    b_refs = refs[1:2 * n:2]
    if split:
        joined = refs[2 * n + n_extra + 1:]

        @pl.when(pl.program_id(0) == 0)
        def _():
            for ref, whole in zip(b_refs, joined):
                join_halves(ref, whole)

        b_refs = joined
    acc = None
    for i, transposed in enumerate(modes):
        part = (dot_nt if transposed else dot_nn)(refs[2 * i][...], b_refs[i][...])
        acc = part if acc is None else acc + part
    extra = [r[...] for r in refs[2 * n:2 * n + n_extra]]
    out[...] = (combine(acc, *extra) if combine is not None else acc).astype(out.dtype)


def row_matmul(pairs, out_dim, out_dtype, extra=(), combine=None, split=False, tm=512):
    n_tok = pairs[0][0].shape[0]
    in_specs, args, scratch, flops, nbytes = [], [], [], 0, 0
    for a, b, transposed, off in pairs:
        k = a.shape[1]
        in_specs.append(pl.BlockSpec((tm, k), lambda t: (t, 0)))
        shape = (out_dim, k) if transposed else (k, out_dim)
        if split:
            scratch.append(pltpu.VMEM(shape, BF))
            in_specs.append(pl.BlockSpec(b.shape, lambda t: (0, 0, 0, 0), pipeline_mode=pl.Buffered(1)))
        else:
            in_specs.append(pl.BlockSpec(shape, lambda t, i=off // shape[1]: (0, i), pipeline_mode=pl.Buffered(1)))
        args += [a, b]
        flops += 2 * n_tok * k * out_dim
        nbytes += 2 * n_tok * k + 2 * k * out_dim
    for e in extra:
        in_specs.append(pl.BlockSpec((tm, out_dim), lambda t: (t, 0)))
        args.append(e)
        nbytes += e.size * e.dtype.itemsize
    return pl.pallas_call(
        functools.partial(mm_kernel, [p[2] for p in pairs], len(extra), combine, split),
        grid=(n_tok // tm,),
        in_specs=in_specs,
        out_specs=pl.BlockSpec((tm, out_dim), lambda t: (t, 0)),
        out_shape=jax.ShapeDtypeStruct((n_tok, out_dim), out_dtype),
        scratch_shapes=scratch,
        compiler_params=params('arbitrary'),
        cost_estimate=cost(flops, nbytes + n_tok * out_dim * jnp.dtype(out_dtype).itemsize),
    )(*args)


def copy_kernel(src, dst):
    dst[...] = src[...]


def copy_out(x):
    rows, cols = x.shape
    block = pl.BlockSpec((rows // 8, cols), lambda i: (i, 0))
    return pl.pallas_call(
        copy_kernel,
        grid=(8,),
        in_specs=[block],
        out_specs=block,
        out_shape=jax.ShapeDtypeStruct(x.shape, x.dtype),
        compiler_params=params('arbitrary'),
        cost_estimate=cost(rows * cols, 8 * rows * cols),
    )(x)


def grad_kernel(spans, layout, *refs):
    n_a = len(spans)
    n_b = sum(len(s) for s in spans)
    a_refs, b_refs = refs[:n_a], refs[n_a:n_a + n_b]
    out_ref, a_t = refs[n_a + n_b], refs[n_a + n_b + 1]
    j = pl.program_id(0)
    i = 0
    for a, group in enumerate(spans):
        @pl.when(j == group[0][0])
        def _(a=a):
            a_t[...] = a_refs[a][...].T

        for lo, hi in group:
            @pl.when((j >= lo) & (j < hi))
            def _(i=i):
                g = dot_nn(a_t[...], b_refs[i][...])
                if layout == 'plain':
                    out_ref[...] = g
                elif layout == 'rows':
                    n_s, part = out_ref.shape[1], out_ref.shape[2]
                    for s in range(n_s):
                        for h in range(2):
                            lo_row = (s * 2 + h) * part
                            out_ref[h, s] = g[lo_row:lo_row + part]
                else:
                    g = g.T
                    n_s, part = out_ref.shape[1], out_ref.shape[2]
                    for s in range(n_s):
                        for h in range(2):
                            lo_row = (s * 2 + h) * part
                            out_ref[h, s] = g[lo_row:lo_row + part]

            i += 1


def weight_grads(groups, layout='plain', nb=768, n_dest=8):
    n_tok, dim = groups[0][0].shape
    spans, a_list, b_list, b_specs, lo = [], [], [], [], 0
    for a, bs in groups:
        a_list.append(a)
        span = []
        for b in bs:
            n = b.shape[1] // nb
            span.append((lo, lo + n))
            b_specs.append(pl.BlockSpec((n_tok, nb), lambda j, lo=lo, n=n: (0, jnp.clip(j - lo, 0, n - 1))))
            b_list.append(b)
            lo += n
        spans.append(span)
    total = lo * nb
    if layout == 'plain':
        out_spec = pl.BlockSpec((dim, nb), lambda j: (0, j))
        out_shape = (dim, total)
    elif layout == 'rows':
        out_spec = pl.BlockSpec((2, n_dest, dim // (2 * n_dest), nb), lambda j: (0, 0, 0, j))
        out_shape = (2, n_dest, dim // (2 * n_dest), total)
    else:
        part = total // (2 * n_dest)
        out_spec = pl.BlockSpec((2, nb // (2 * part), part, dim), lambda j: (0, j, 0, 0))
        out_shape = (2, n_dest, part, dim)
    return pl.pallas_call(
        functools.partial(grad_kernel, spans, layout),
        grid=(lo,),
        in_specs=[pl.BlockSpec((n_tok, dim), lambda j: (0, 0), pipeline_mode=pl.Buffered(1))] * len(a_list) + b_specs,
        out_specs=out_spec,
        out_shape=jax.ShapeDtypeStruct(out_shape, F32),
        scratch_shapes=[pltpu.VMEM((dim, n_tok), BF)],
        compiler_params=params('arbitrary'),
        cost_estimate=cost(2 * n_tok * dim * total, 2 * n_tok * (dim + total) + 4 * dim * total),
    )(*a_list, *b_list)


def rms_scale(tokens):
    return lax.rsqrt(jnp.mean(tokens * tokens, axis=-1, keepdims=True) + EPS_NORM)


def rms_back(d_norm, tokens, inv_rms, gamma_vec):
    scaled = d_norm * gamma_vec
    dot = jnp.mean(scaled * tokens, axis=-1, keepdims=True)
    d_tokens = inv_rms * scaled - tokens * (inv_rms * inv_rms * inv_rms * dot)
    d_gamma = jnp.sum(d_norm * (tokens * inv_rms), axis=0)
    return d_tokens, d_gamma


def route_slots(flat_ids, n_experts, capacity):
    onehot = flat_ids[:, None] == jnp.arange(n_experts)[None, :]
    running = jnp.cumsum(onehot.astype(jnp.int32), axis=0)
    slot_idx = jnp.sum(jnp.where(onehot, running, 0), axis=1) - 1
    return onehot, flat_ids * capacity + slot_idx


def exchange(x, axes):
    return lax.all_to_all(x, axes, 0, 0, tiled=True)


def to_expert(rows, n_dev):
    n_slots, dim = rows.shape
    return exchange(rows.reshape(n_dev, n_slots // n_dev, dim), ALL_AXES).reshape(n_slots, dim)


def fetch_expert(w_block, n_fsdp):
    e_local, rows, cols = w_block.shape
    mine = exchange(w_block.reshape(n_fsdp, rows * e_local // n_fsdp, cols), 'fsdp')
    return lax.all_gather(mine, 'fsdp', axis=0, tiled=False, axis_index_groups=PAIRS)


def return_grad(grad, e_local):
    n_fsdp = grad.shape[1]
    summed = lax.psum_scatter(grad, 'fsdp', scatter_dimension=0, tiled=False, axis_index_groups=PAIRS)
    back = exchange(summed, 'fsdp')
    rows, cols = summed.shape[1:]
    return copy_out(back.reshape(n_fsdp * rows, cols)).reshape(e_local, n_fsdp // e_local * rows, cols)


def spread(rows, dest_row, n_slots):
    return jnp.zeros((n_slots, rows.shape[1]), BF).at[dest_row].set(rows, unique_indices=True, mode='promise_in_bounds')


def device_step(n_dev, n_fsdp, x_in, grad_y, w_q, w_k, w_v, w_o, gamma_attn, gamma_mlp, w_router, w1_shared, w3_shared, w2_shared, w1_expert, w3_expert, w2_expert, expert_ids):
    n_batch, seq_len, dim = x_in.shape
    n_tok = n_batch * seq_len
    n_heads = w_q.shape[1]
    width = n_heads * HEAD
    n_experts = w_router.shape[1]
    e_local = w1_expert.shape[0]
    ff = w1_shared.shape[1]
    ff_e = w1_expert.shape[2]
    shard = w_q.shape[0]
    capacity = 2 * n_tok // n_experts
    n_slots = n_experts * capacity

    small = jnp.concatenate([w_router, gamma_attn.astype(F32)[:, None], gamma_mlp.astype(F32)[:, None]], axis=1)
    small = exchange(jnp.broadcast_to(small.reshape(1, 1, small.size), (n_dev, 1, small.size)), ALL_AXES).reshape(dim, n_experts + 2)
    wr, ga, gm = small[:, :n_experts], small[:, n_experts], small[:, n_experts + 1]
    w_attn = jnp.concatenate([w_q.reshape(shard, width), w_k.reshape(shard, width), w_v.reshape(shard, width), w_o.reshape(width, shard).T], axis=1)
    w_attn = lax.all_gather(w_attn, ALL_AXES, axis=0, tiled=True)
    w_sh = jnp.concatenate([w1_shared, w3_shared, w2_shared.T], axis=1)
    w_sh = lax.all_gather(w_sh, ALL_AXES, axis=0, tiled=True)
    w1e, w3e, w2e = (fetch_expert(w, n_fsdp) for w in (w1_expert, w3_expert, w2_expert))

    onehot, dest_row = route_slots(expert_ids.reshape(n_tok), n_experts, capacity)
    d_out = grad_y.reshape(n_tok, dim)
    d_down = to_expert(spread(d_out, dest_row, n_slots), n_dev)

    tables = head_tables(seq_len)
    tokens = x_in.reshape(n_tok, dim)
    tok_f = tokens.astype(F32)
    inv1 = rms_scale(tok_f)
    normed1 = (tok_f * inv1 * ga).astype(BF)
    qkv = jnp.dot(normed1, w_attn[:, :3 * width], preferred_element_type=F32).astype(BF)
    attn = []
    for b in range(n_batch):
        attn = attn_fwd(qkv, tables, seq_len, attn, b, b + 1)
    attn = attn[0]
    attn_out = dot_nt(attn, w_attn[:, 3 * width:])
    hidden = (tok_f + attn_out).astype(BF)
    hid_f = hidden.astype(F32)
    inv2 = rms_scale(hid_f)
    normed2 = (hid_f * inv2 * gm).astype(BF)
    normed2_f = normed2.astype(F32)
    logits = jnp.dot(normed2, wr, preferred_element_type=F32, precision=lax.Precision.HIGHEST)
    gate_val = jax.nn.sigmoid(jnp.sum(jnp.where(onehot, logits, 0.0), axis=1))
    routed_in = (gate_val[:, None] * normed2_f).astype(BF)
    rows = to_expert(spread(routed_in, dest_row, n_slots), n_dev)

    act_s, dg_s, dl_s = swiglu(normed2, d_out, w_sh, ff, False)
    base = row_matmul([(act_s, w_sh, True, 2 * ff)], dim, F32, extra=(hidden,), combine=lambda acc, h: h.astype(F32) + acc)
    d_n2_shared = row_matmul([(dg_s, w_sh, True, 0), (dl_s, w_sh, True, ff)], dim, F32)
    g_sh = weight_grads([(normed2, [dg_s, dl_s]), (d_out, [act_s])])
    g_sh = lax.psum_scatter(g_sh, ALL_AXES, scatter_dimension=0, tiled=True)

    act_e, dg_e, dl_e = swiglu(rows, d_down, (w1e, w3e, w2e), ff_e, True)
    d_rows = row_matmul([(dg_e, w1e, True, 0), (dl_e, w3e, True, 0)], dim, BF, split=True)
    d_back = to_expert(d_rows, n_dev)
    down = row_matmul([(act_e, w2e, False, 0)], dim, BF, split=True)
    back = to_expert(down, n_dev)
    g_w2e = return_grad(weight_grads([(d_down, [act_e])], 'cols', n_dest=n_fsdp), e_local)
    g_w1e = return_grad(weight_grads([(rows, [dg_e])], 'rows', n_dest=n_fsdp), e_local)
    g_w3e = return_grad(weight_grads([(rows, [dl_e])], 'rows', n_dest=n_fsdp), e_local)
    routed = back.at[dest_row].get(mode='promise_in_bounds').astype(F32)
    layer_out = (base + routed).astype(BF)

    d_routed = d_back.at[dest_row].get(mode='promise_in_bounds').astype(F32)
    d_gate = jnp.sum(d_routed * normed2_f, axis=1) * gate_val * (1.0 - gate_val)
    d_logits = jnp.where(onehot, d_gate[:, None], 0.0)
    g_wr = jnp.einsum('td,te->de', normed2_f, d_logits, precision=lax.Precision.HIGHEST)
    d_n2 = d_n2_shared + gate_val[:, None] * d_routed + jnp.einsum('te,de->td', d_logits, wr, precision=lax.Precision.HIGHEST)
    d_hid, g_gm = rms_back(d_n2.astype(BF).astype(F32), hid_f, inv2, gm)
    d_hidden = (d_out.astype(F32) + d_hid.astype(BF).astype(F32)).astype(BF)

    d_attn = jnp.dot(d_hidden, w_attn[:, 3 * width:], preferred_element_type=F32).astype(BF)
    d_qkv = []
    for b in range(n_batch):
        d_qkv = attn_bwd(qkv, d_attn, tables, seq_len, d_qkv, b, b + 1)
    d_q, d_k, d_v = d_qkv
    g_attn = weight_grads([(normed1, [d_q, d_k, d_v]), (d_hidden, [attn])])
    g_attn = lax.psum_scatter(g_attn, ALL_AXES, scatter_dimension=0, tiled=True)
    d_n1 = row_matmul([(d_q, w_attn, True, 0), (d_k, w_attn, True, width), (d_v, w_attn, True, 2 * width)], dim, F32)
    d_tok, g_ga = rms_back(d_n1.astype(BF).astype(F32), tok_f, inv1, ga)
    d_x = (d_hidden.astype(F32) + d_tok.astype(BF).astype(F32)).astype(BF)

    tiny = jnp.concatenate([g_wr, g_ga[:, None], g_gm[:, None]], axis=1).reshape(n_dev, shard, n_experts + 2)
    tiny = jnp.sum(exchange(tiny, ALL_AXES), axis=0)

    g_q, g_k, g_v = (g_attn[:, i * width:(i + 1) * width].reshape(shard, n_heads, HEAD) for i in range(3))
    g_o = g_attn[:, 3 * width:].T.reshape(n_heads, HEAD, shard)
    return (layer_out.reshape(x_in.shape), d_x.reshape(x_in.shape), g_q, g_k, g_v, g_o, tiny[:, n_experts], tiny[:, n_experts + 1], tiny[:, :n_experts],
            g_sh[:, :ff], g_sh[:, ff:2 * ff], g_sh[:, 2 * ff:].T, g_w1e, g_w3e, g_w2e)


def solution(mesh):
    tok_spec = P(ALL_AXES, None, None)
    mat_spec = P(ALL_AXES, None)
    vec_spec = P(ALL_AXES)
    wo_spec = P(None, None, ALL_AXES)
    w2s_spec = P(None, ALL_AXES)
    exp_spec = P('ep', 'fsdp', None)
    in_specs = (tok_spec, tok_spec, tok_spec, tok_spec, tok_spec, wo_spec, vec_spec, vec_spec, mat_spec, mat_spec, mat_spec, w2s_spec, exp_spec, exp_spec, exp_spec, mat_spec)
    out_specs = (tok_spec, tok_spec, tok_spec, tok_spec, tok_spec, wo_spec, vec_spec, vec_spec, mat_spec, mat_spec, mat_spec, w2s_spec, exp_spec, exp_spec, exp_spec)

    def step(*args):
        return device_step(mesh.size, mesh.shape['fsdp'], *args)

    return jax.shard_map(step, mesh=mesh, in_specs=in_specs, out_specs=out_specs, check_vma=False)
```

time: 2060 us -> 1290 us (0.63)
  matrix products: 792 us -> 39.9 us
  Pallas kernels: 0 us -> 558 us
  waiting for transfers between devices: 825 us -> 402 us
  local copies, waits for them, and re-layouts: 183 us -> 64.3 us
  other arithmetic: 129 us -> 48.3 us
  blocking collectives: 80.2 us -> 120 us
    dot_general x46 -> x6, matrix products: 788 us -> 39.9 us  [the longest x1 12.4 us: device_step(): jnp.einsum('te,de->td', d_logits, wr, precision=lax.Precision.HIGHEST)]
    reduce_scatter x10 -> x5, waiting for transfers between devices: 596 us -> 0.05 us  [the longest x3 0.04 us: return_grad(): lax.psum_scatter(grad, 'fsdp', scatter_dimension=0, tiled=False, axis_ind...]
    pallas_call x0 -> x23, Pallas kernels: none -> 558 us  [the longest x5 150 us: weight_grads(): pl.pallas_call(functools.partial(grad_kernel, spans, layout), grid=(lo,),...]
    all_to_all x4 -> x8, waiting for transfers between devices: 199 us -> 402 us  [exchange(): return lax.all_to_all(x, axes, 0, 0, tiled=True)]
    all_to_all x0 -> x4, blocking collectives: none -> 120 us  [exchange(): return lax.all_to_all(x, axes, 0, 0, tiled=True)]
    unnamed x2 -> x0, blocking collectives: 67.4 us -> none
    reduce_sum x9 -> x4, other arithmetic: 68 us -> 7.99 us  [the longest x1 4.08 us: rms_back(): d_gamma = jnp.sum(d_norm * (tokens * inv_rms), axis=0)]
    convert_element_type x6 -> x0, local copies, waits for them, and re-layouts: 43.2 us -> none  [the longest x2 17.1 us: rope_norm(): return rotated.astype(jnp.bfloat16)]
  transfers between devices with their start and end apart: 25 -> 18, of which waited for: 8 -> 6; matrix products, arithmetic and copies ran while one was open for 52% -> 11% of each run, Pallas kernels for 0% -> 44%
where the time goes in v1:
time: 1290 us; the launch traced here: 1280 us
  Pallas kernels  558 us (43%)
  waiting for transfers between devices  402 us (31%)
  blocking collectives  120 us (9%)
  local copies, waits for them, and re-layouts  64.3 us (5%)
  other arithmetic  48.3 us (4%)
  matrix products  39.9 us (3%)
  starting transfers between devices  33.7 us (3%)
  between operations  15.2 us (1%)
    all_to_all x8, waiting for transfers between devices, exchange(): return lax.all_to_all(x, axes, 0, 0, tiled=True)  402 us
    pallas_call x5, Pallas kernels, weight_grads(): pl.pallas_call(functools.partial(grad_kernel, spans, layout), grid=(lo,),...  150 us
    pallas_call x8, Pallas kernels, attn_call(): pl.pallas_call(kernel, grid=(hi - lo, groups), in_specs=[block(off) for o...  147 us
    pallas_call x5, Pallas kernels, row_matmul(): pl.pallas_call(functools.partial(mm_kernel, [p[2] for p in pairs], len(ex...  129 us
    all_to_all x4, blocking collectives, exchange(): return lax.all_to_all(x, axes, 0, 0, tiled=True)  120 us
    pallas_call x2, Pallas kernels, swiglu(): pl.pallas_call(functools.partial(swiglu_kernel, chunk, split), grid=(widt...  111 us
    all_to_all x8, starting transfers between devices, exchange(): return lax.all_to_all(x, axes, 0, 0, tiled=True)  33.3 us
  transfers between devices with their start and end apart: 18, of which 6 were waited for; matrix products, arithmetic and copies ran while one was open for 11% of the time, Pallas kernels for 44%

profile of v1, /device:TPU:0, one launch (start us, length us, event | category | flops | bytes accessed | tf_op | source)
XLA Modules:
  0.0 1281.8 jit_solution(12703531752282876558)
XLA Ops:
  12.7 41.0 %all_to_all.60 = bf16[8,48,3072]{2,1,0:T(8,128)(2,1)} all-to-all(bf16[8,48,3072]{2,1,0:T(8,128)(2,1)S(1)} %bitcast.119), channel_id=1, replica_groups=mesh['ep'=2,'fsdp'=8] {'fsdp'}, dimensions={0} | all-to-all | bytes 4718592 | tf_op jit(solution)/shard_map/all_to_all | solution.py:397
  53.8 36.1 %all_to_all.61 = bf16[8,48,3072]{2,1,0:T(8,128)(2,1)} all-to-all(bf16[8,48,3072]{2,1,0:T(8,128)(2,1)} %bitcast.120), channel_id=1, replica_groups=mesh['ep'=2,'fsdp'=8] {'fsdp'}, dimensions={0} | all-to-all | bytes 4718592 | tf_op jit(solution)/shard_map/all_to_all | solution.py:397
  90.0 34.0 %all_to_all.62 = bf16[8,192,768]{2,1,0:T(8,128)(2,1)} all-to-all(bf16[8,192,768]{2,1,0:T(8,128)(2,1)} %bitcast.121), channel_id=1, replica_groups=mesh['ep'=2,'fsdp'=8] {'fsdp'}, dimensions={0} | all-to-all | bytes 4718592 | tf_op jit(solution)/shard_map/all_to_all | solution.py:397
  135.4 14.1 %scatter_custom_fusion.1 = bf16[4096,768]{1,0:T(8,128)(2,1)} fusion(s32[2048]{0:T(1024)S(1)} %bitcast.133, bf16[2048,768]{1,0:T(8,128)(2,1)} %bitcast.115, bf16[]{:T(256)} %constant.28.clone.1), kind=kCustom, calls=%fused_computation.50 | custom fusion | bytes 6291968 | tf_op jit(solution)/shard_map/scatter | solution.py:420
  171.9 14.6 %shard_map.271.rest_0_ = bf16[2048,768]{1,0:T(8,128)(2,1)} custom-call(bf16[2048,2304]{1,0:T(8,128)(2,1)} %convolution_convert_fusion.q_ref.k_ref.v_ref, bf16[2048,2304]{1,0:T(8,128)(2,1)} %convolution_convert_fusion.q_ref.k_ref.v_ref, bf16[2048,2304]{1,0:T(8,128)(2,1)} %convolution_convert_fusion.q_ref.k_ref.v_ref, f32[512,128]{1,0:T(8,128)} %get-tuple-element.119.cos_ref, ...), custom_call_target="tpu_custom_call" | custom-call | flops 4026531840 | bytes 3145728 | tf_op jit(solution)/shard_map/pallas_call | solution.py:157
  186.5 14.6 %shard_map.272.rest_0_ = bf16[2048,768]{1,0:T(8,128)(2,1)} custom-call(bf16[2048,2304]{1,0:T(8,128)(2,1)} %convolution_convert_fusion.q_ref.k_ref.v_ref, bf16[2048,2304]{1,0:T(8,128)(2,1)} %convolution_convert_fusion.q_ref.k_ref.v_ref, bf16[2048,2304]{1,0:T(8,128)(2,1)} %convolution_convert_fusion.q_ref.k_ref.v_ref, ...), custom_call_target="tpu_custom_call", output_to_operand_aliasing={{}: (5, {})} | custom-call | flops 4026531840 | bytes 3145728 | tf_op jit(solution)/shard_map/pallas_call | solution.py:157
  201.1 14.6 %shard_map.273.rest_0_ = bf16[2048,768]{1,0:T(8,128)(2,1)} custom-call(bf16[2048,2304]{1,0:T(8,128)(2,1)} %convolution_convert_fusion.q_ref.k_ref.v_ref, bf16[2048,2304]{1,0:T(8,128)(2,1)} %convolution_convert_fusion.q_ref.k_ref.v_ref, bf16[2048,2304]{1,0:T(8,128)(2,1)} %convolution_convert_fusion.q_ref.k_ref.v_ref, ...), custom_call_target="tpu_custom_call", output_to_operand_aliasing={{}: (5, {})} | custom-call | flops 4026531840 | bytes 3145728 | tf_op jit(solution)/shard_map/pallas_call | solution.py:157
  215.8 14.8 %shard_map.274.refs_5_ = bf16[2048,768]{1,0:T(8,128)(2,1)} custom-call(bf16[2048,2304]{1,0:T(8,128)(2,1)} %convolution_convert_fusion.q_ref.k_ref.v_ref, bf16[2048,2304]{1,0:T(8,128)(2,1)} %convolution_convert_fusion.q_ref.k_ref.v_ref, bf16[2048,2304]{1,0:T(8,128)(2,1)} %convolution_convert_fusion.q_ref.k_ref.v_ref, ...), custom_call_target="tpu_custom_call", output_to_operand_aliasing={{}: (5, {})} | custom-call | flops 4026531840 | bytes 3145728 | tf_op jit(solution)/shard_map/pallas_call | solution.py:157
  243.0 14.2 %scatter_custom_fusion = bf16[4096,768]{1,0:T(8,128)(2,1)} fusion(s32[2048]{0:T(1024)} %bitcast.134, f32[2048]{0:T(1024)S(1)} %add_divide_fusion, bf16[]{:T(256)} %constant.28.clone.1, bf16[2048,768]{1,0:T(8,128)(2,1)S(1)} %get-tuple-element.115.refs_2_, f32[768]{0:T(1024)} %get-tuple-element.100, f32[2048]{0:T(1024)S(1)} %add_rsqrt_fusion), kind=kCustom, calls=%fused_computation.48 | custom fusion | flops 11010048 | bytes 9458176 | tf_op jit(solution)/shard_map/scatter | solution.py:420
  261.3 77.6 %all-to-all-done.1 = bf16[16,256,768]{2,1,0:T(8,128)(2,1)} async-done(((bf16[16,256,768]{2,1,0:T(8,128)(2,1)}), bf16[16,256,768]{2,1,0:T(8,128)(2,1)}, u32[]{:S(2)}, u32[]{:S(2)}) %all-to-all-start.1) | async-done | bytes 6291488 | tf_op jit(solution)/shard_map/all_to_all | solution.py:397
  338.9 72.5 %shard_map.277 = (bf16[4096,3072]{1,0:T(8,128)(2,1)}, bf16[4096,3072]{1,0:T(8,128)(2,1)}, bf16[4096,3072]{1,0:T(8,128)(2,1)}) custom-call(bf16[4096,768]{1,0:T(8,128)(2,1)} %bitcast.10.x_ref.refs_0_, bf16[4096,768]{1,0:T(8,128)(2,1)} %bitcast.12.dy_ref.refs_0_, bf16[2,8,48,3072]{3,2,1,0:T(8,128)(2,1)} %bitcast.141, bf16[2,8,48,3072]{3,2,1,0:T(8,128)(2,1)} %bitcast.143, ...), custom_call_target="tpu_custom_call" | custom-call | flops 57982058496 | bytes 114819072 | tf_op jit(solution)/shard_map/pallas_call | solution.py:224
  411.3 29.1 %shard_map.292 = f32[2,8,192,768]{3,2,1,0:T(8,128)} custom-call(bf16[4096,768]{1,0:T(8,128)(2,1)} %bitcast.12.dy_ref.refs_0_, bf16[4096,3072]{1,0:T(8,128)(2,1)} %get-tuple-element.34.refs_0_.refs_1_), custom_call_target="tpu_custom_call" | custom-call | flops 19327352832 | bytes 40894464 | tf_op jit(solution)/shard_map/pallas_call | solution.py:365
  440.5 28.3 %shard_map.288 = f32[2,8,48,3072]{3,2,1,0:T(8,128)} custom-call(bf16[4096,768]{1,0:T(8,128)(2,1)} %bitcast.10.x_ref.refs_0_, bf16[4096,3072]{1,0:T(8,128)(2,1)} %get-tuple-element.37.refs_0_.refs_1_), custom_call_target="tpu_custom_call" | custom-call | flops 19327352832 | bytes 40894464 | tf_op jit(solution)/shard_map/pallas_call | solution.py:365
  468.9 28.7 %shard_map.290 = f32[2,8,48,3072]{3,2,1,0:T(8,128)} custom-call(bf16[4096,768]{1,0:T(8,128)(2,1)} %bitcast.10.x_ref.refs_0_, bf16[4096,3072]{1,0:T(8,128)(2,1)} %get-tuple-element.38.refs_2_.refs_1_), custom_call_target="tpu_custom_call" | custom-call | flops 19327352832 | bytes 40894464 | tf_op jit(solution)/shard_map/pallas_call | solution.py:365
  497.6 47.7 %shard_map.280 = bf16[4096,768]{1,0:T(8,128)(2,1)} custom-call(bf16[4096,3072]{1,0:T(8,128)(2,1)} %get-tuple-element.37.refs_0_.refs_1_, bf16[2,8,48,3072]{3,2,1,0:T(8,128)(2,1)} %bitcast.142, bf16[4096,3072]{1,0:T(8,128)(2,1)} %get-tuple-element.38.refs_2_.refs_1_, bf16[2,8,48,3072]{3,2,1,0:T(8,128)(2,1)} %bitcast.144), custom_call_target="tpu_custom_call" | custom-call | flops 38654705664 | bytes 66060288 | tf_op jit(solution)/shard_map/pallas_call | solution.py:276
  550.4 77.2 %all-to-all-done.7 = bf16[16,256,768]{2,1,0:T(8,128)(2,1)} async-done(((bf16[16,256,768]{2,1,0:T(8,128)(2,1)}), bf16[16,256,768]{2,1,0:T(8,128)(2,1)}, u32[]{:S(2)}, u32[]{:S(2)}) %all-to-all-start.7) | async-done | bytes 6291488 | tf_op jit(solution)/shard_map/all_to_all | solution.py:397
  627.6 14.0 %gather_fusion.1 = bf16[2048,768]{1,0:T(8,128)(2,1)} fusion(bf16[4096,768]{1,0:T(8,128)(2,1)} %bitcast.23, s32[2048]{0:T(1024)S(1)} %broadcast_clamp_fusion), kind=kCustom, calls=%fused_computation.1 | custom fusion | bytes 6299648 | tf_op jit(solution)/shard_map/gather | solution.py:487
  645.5 38.7 %shard_map.275 = (bf16[2048,3072]{1,0:T(8,128)(2,1)}, bf16[2048,3072]{1,0:T(8,128)(2,1)}, bf16[2048,3072]{1,0:T(8,128)(2,1)}) custom-call(bf16[2048,768]{1,0:T(8,128)(2,1)} %copy-done.4, bf16[2048,768]{1,0:T(8,128)(2,1)} %bitcast.116, bf16[768,9216]{1,0:T(8,128)(2,1)} %all-gather.11.cloned.1.call-done.w1_ref.w3_ref.w2_ref.refs_1_.refs_3_, ...), custom_call_target="tpu_custom_call" | custom-call | flops 28991029248 | bytes 64487424 | tf_op jit(solution)/shard_map/pallas_call | solution.py:224
  684.1 27.1 %shard_map.279 = f32[2048,768]{1,0:T(8,128)} custom-call(bf16[2048,3072]{1,0:T(8,128)(2,1)} %get-tuple-element.35.refs_0_.refs_2_, bf16[768,9216]{1,0:T(8,128)(2,1)} %all-gather.11.cloned.1.call-done.w1_ref.w3_ref.w2_ref.refs_1_.refs_3_, bf16[2048,3072]{1,0:T(8,128)(2,1)} %get-tuple-element.36.refs_2_.refs_3_, ...), custom_call_target="tpu_custom_call" | custom-call | flops 19327352832 | bytes 40894464 | tf_op jit(solution)/shard_map/pallas_call | solution.py:276
  732.7 22.1 %shard_map.281 = (bf16[2048,768]{1,0:T(8,128)(2,1)}, bf16[2048,768]{1,0:T(8,128)(2,1)}, bf16[2048,768]{1,0:T(8,128)(2,1)}) custom-call(bf16[2048,2304]{1,0:T(8,128)(2,1)} %convolution_convert_fusion.q_ref.k_ref.v_ref, bf16[2048,2304]{1,0:T(8,128)(2,1)} %convolution_convert_fusion.q_ref.k_ref.v_ref, ...), custom_call_target="tpu_custom_call" | custom-call | flops 10066329600 | bytes 5505024 | tf_op jit(solution)/shard_map/pallas_call | solution.py:157
  754.8 22.4 %shard_map.282 = (bf16[2048,768]{1,0:T(8,128)(2,1)}, bf16[2048,768]{1,0:T(8,128)(2,1)}, bf16[2048,768]{1,0:T(8,128)(2,1)}) custom-call(bf16[2048,2304]{1,0:T(8,128)(2,1)} %convolution_convert_fusion.q_ref.k_ref.v_ref, bf16[2048,2304]{1,0:T(8,128)(2,1)} %convolution_convert_fusion.q_ref.k_ref.v_ref, ...), custom_call_target="tpu_custom_call", output_to_operand_aliasing={{0}: (6, {}), {1}: (7, {}), {2}: (8, {})} | custom-call | flops 10066329600 | bytes 5505024 | tf_op jit(solution)/shard_map/pallas_call | solution.py:157
  777.2 22.2 %shard_map.283 = (bf16[2048,768]{1,0:T(8,128)(2,1)}, bf16[2048,768]{1,0:T(8,128)(2,1)}, bf16[2048,768]{1,0:T(8,128)(2,1)}) custom-call(bf16[2048,2304]{1,0:T(8,128)(2,1)} %convolution_convert_fusion.q_ref.k_ref.v_ref, bf16[2048,2304]{1,0:T(8,128)(2,1)} %convolution_convert_fusion.q_ref.k_ref.v_ref, ...), custom_call_target="tpu_custom_call", output_to_operand_aliasing={{0}: (6, {}), {1}: (7, {}), {2}: (8, {})} | custom-call | flops 10066329600 | bytes 5505024 | tf_op jit(solution)/shard_map/pallas_call | solution.py:157
  799.4 22.1 %shard_map.284 = (bf16[2048,768]{1,0:T(8,128)(2,1)}, bf16[2048,768]{1,0:T(8,128)(2,1)}, bf16[2048,768]{1,0:T(8,128)(2,1)}) custom-call(bf16[2048,2304]{1,0:T(8,128)(2,1)} %convolution_convert_fusion.q_ref.k_ref.v_ref, bf16[2048,2304]{1,0:T(8,128)(2,1)} %convolution_convert_fusion.q_ref.k_ref.v_ref, ...), custom_call_target="tpu_custom_call", output_to_operand_aliasing={{0}: (6, {}), {1}: (7, {}), {2}: (8, {})} | custom-call | flops 10066329600 | bytes 5505024 | tf_op jit(solution)/shard_map/pallas_call | solution.py:157
  821.5 20.8 %shard_map.286 = f32[768,3072]{1,0:T(8,128)} custom-call(bf16[2048,768]{1,0:T(8,128)(2,1)} %fusion.20.refs_0_, bf16[2048,768]{1,0:T(8,128)(2,1)} %copy-done.6, bf16[2048,768]{1,0:T(8,128)(2,1)} %get-tuple-element.48.refs_0_.refs_2_, bf16[2048,768]{1,0:T(8,128)(2,1)} %get-tuple-element.49.refs_2_.refs_3_, bf16[2048,768]{1,0:T(8,128)(2,1)} %get-tuple-element.50.refs_4_, ...), custom_call_target="tpu_custom_call" | custom-call | flops 9663676416 | bytes 25165824 | tf_op jit(solution)/shard_map/pallas_call | solution.py:365
  842.4 43.1 %shard_map.287 = f32[768,9216]{1,0:T(8,128)} custom-call(bf16[2048,768]{1,0:T(8,128)(2,1)} %copy-done.4, bf16[2048,768]{1,0:T(8,128)(2,1)} %bitcast.117, bf16[2048,3072]{1,0:T(8,128)(2,1)} %get-tuple-element.35.refs_0_.refs_2_, bf16[2048,3072]{1,0:T(8,128)(2,1)} %get-tuple-element.36.refs_2_.refs_3_, bf16[2048,3072]{1,0:T(8,128)(2,1)} %get-tuple-element.33.refs_0_.refs_4_), custom_call_target="tpu_custom_call" | custom-call | flops 28991029248 | bytes 69206016 | tf_op jit(solution)/shard_map/pallas_call | solution.py:365
  885.5 26.0 %shard_map.278 = bf16[4096,768]{1,0:T(8,128)(2,1)} custom-call(bf16[4096,3072]{1,0:T(8,128)(2,1)} %get-tuple-element.34.refs_0_.refs_1_, bf16[2,8,192,768]{3,2,1,0:T(8,128)(2,1)} %bitcast.140), custom_call_target="tpu_custom_call" | custom-call | flops 19327352832 | bytes 36175872 | tf_op jit(solution)/shard_map/pallas_call | solution.py:276
  917.1 12.6 shard_map.285
  934.1 62.4 %all-to-all-done.6 = bf16[16,256,768]{2,1,0:T(8,128)(2,1)} async-done(((bf16[16,256,768]{2,1,0:T(8,128)(2,1)}), bf16[16,256,768]{2,1,0:T(8,128)(2,1)}, u32[]{:S(2)}, u32[]{:S(2)}) %all-to-all-start.6) | async-done | bytes 6291488 | tf_op jit(solution)/shard_map/all_to_all | solution.py:397
  1010.1 97.1 %all-to-all-done.11 = f32[8,192,768]{2,1,0:T(8,128)} async-done(((f32[8,192,768]{2,1,0:T(8,128)}), f32[8,192,768]{2,1,0:T(8,128)}, u32[]{:S(2)}, u32[]{:S(2)}) %all-to-all-start.11) | async-done | bytes 4718624 | tf_op jit(solution)/shard_map/all_to_all | solution.py:397
  1111.8 78.7 %all-to-all-done.9 = f32[8,48,3072]{2,1,0:T(8,128)} async-done(((f32[8,48,3072]{2,1,0:T(8,128)}), f32[8,48,3072]{2,1,0:T(8,128)}, u32[]{:S(2)}, u32[]{:S(2)}) %all-to-all-start.9) | async-done | bytes 4718624 | tf_op jit(solution)/shard_map/all_to_all | solution.py:397
  1195.2 13.7 %gather_fusion = bf16[2048,768]{1,0:T(8,128)(2,1)} fusion(bf16[4096,768]{1,0:T(8,128)(2,1)} %bitcast.20, s32[2048]{0:T(1024)S(1)} %copy-done.26), kind=kCustom, calls=%fused_computation | custom fusion | bytes 6299648 | tf_op jit(solution)/shard_map/gather | solution.py:484
  1208.9 15.4 %shard_map.276 = f32[2048,768]{1,0:T(8,128)} custom-call(bf16[2048,3072]{1,0:T(8,128)(2,1)} %get-tuple-element.33.refs_0_.refs_4_, bf16[768,9216]{1,0:T(8,128)(2,1)} %all-gather.11.cloned.1.call-done.w1_ref.w3_ref.w2_ref.refs_1_.refs_3_, bf16[2048,768]{1,0:T(8,128)(2,1)} %copy-done), custom_call_target="tpu_custom_call" | custom-call | flops 9663676416 | bytes 26738688 | tf_op jit(solution)/shard_map/pallas_call | solution.py:276
  (200 shorter events, 169.1 us)
Async XLA Ops:
  7.2 152.3 %all-gather.9.cloned.1.call-start = ((), (), s32[]{:S(2)}) async-start(), calls=%async_computation.17 | async-start | bytes 5013504 | tf_op jit(solution)/shard_map/all_gather | solution.py:440
  12.6 248.6 %all-gather.13.cloned.1.call-start = ((), (), s32[]{:S(2)}) async-start(), calls=%async_computation.24 | async-start | bytes 7077888 | tf_op jit(solution)/shard_map/all_gather | solution.py:408
  53.7 207.5 %all-gather.15.cloned.1.call-start = ((), (), s32[]{:S(2)}) async-start(), calls=%async_computation.25 | async-start | bytes 7077888 | tf_op jit(solution)/shard_map/all_gather | solution.py:408
  89.9 34.3 %copy-start.12 = (bf16[3072,48]{0,1:T(8,128)(2,1)S(1)}, bf16[3072,48]{0,1:T(8,128)(2,1)}, u32[]{:S(2)}) copy-start(bf16[3072,48]{0,1:T(8,128)(2,1)} %param.27) | copy-start | bytes 884740
  89.9 171.4 %all-gather.17.cloned.1.call-start = ((), (), s32[]{:S(2)}) async-start(), calls=%async_computation.26 | async-start | bytes 7077888 | tf_op jit(solution)/shard_map/all_gather | solution.py:408
  89.9 36.3 %copy-start.37 = (bf16[48]{0:T(256)(128)(2,1)S(1)}, bf16[48]{0:T(256)(128)(2,1)}, u32[]{:S(2)}) copy-start(bf16[48]{0:T(256)(128)(2,1)} %param.23) | copy-start | bytes 292
  90.0 36.3 %copy-start.38 = (bf16[48]{0:T(256)(128)(2,1)S(1)}, bf16[48]{0:T(256)(128)(2,1)}, u32[]{:S(2)}) copy-start(bf16[48]{0:T(256)(128)(2,1)} %param.22) | copy-start | bytes 292
  90.0 36.3 %copy-start.36 = (f32[48,8]{0,1:T(8,128)S(1)}, f32[48,8]{0,1:T(8,128)}, u32[]{:S(2)}) copy-start(f32[48,8]{0,1:T(8,128)} %param.24) | copy-start | bytes 4612
  90.0 39.4 %copy-start.24 = (s32[4,512]{1,0:T(4,128)S(1)}, s32[4,512]{1,0:T(4,128)}, u32[]{:S(2)}) copy-start(s32[4,512]{1,0:T(4,128)} %param.31) | copy-start | bytes 24580
  90.0 42.4 %copy-start.2 = (bf16[4,512,768]{2,1,0:T(8,128)(2,1)S(1)}, bf16[4,512,768]{2,1,0:T(8,128)(2,1)}, u32[]{:S(2)}) copy-start(bf16[4,512,768]{2,1,0:T(8,128)(2,1)} %param.16) | copy-start | bytes 9437188
  124.1 521.4 %all-gather.11.cloned.1.call-start = ((), (), s32[]{:S(2)}) async-start(), calls=%async_computation.18 | async-start | bytes 15040512 | tf_op jit(solution)/shard_map/all_gather | solution.py:442
  127.2 22.4 %all-to-all-start = ((f32[16,1,480]{2,1,0:T(1,128)}), f32[16,1,480]{2,1,0:T(1,128)S(1)}, u32[]{:S(2)}, u32[]{:S(2)}) async-start(f32[16,1,480]{2,1,0:T(1,128)} %broadcast_in_dim.58), calls=%async_computation | async-start | bytes 65536 | tf_op jit(solution)/shard_map/all_to_all | solution.py:397
  129.5 108.7 %copy-start.17 = (s32[1,4,4,128]{3,1,2,0:T(4,128)}, s32[1,4,4,128]{3,1,2,0:T(4,128)S(1)}, u32[]{:S(2)}) copy-start(s32[1,4,4,128]{3,1,2,0:T(4,128)S(1)} %copy.72) | copy-start | bytes 24580
  134.2 15.4 %copy-start.30 = (s32[2048,1]{0,1:T(1,128)}, s32[2048,1]{0,1:T(1,128)S(1)}, u32[]{:S(2)}) copy-start(s32[2048,1]{0,1:T(1,128)S(1)} %compare_select_fusion) | copy-start | bytes 24580
  135.4 21.1 %copy-start.13 = (f32[1,4,4,128]{3,1,2,0:T(4,128)}, f32[1,4,4,128]{3,1,2,0:T(4,128)S(1)}, u32[]{:S(2)}) copy-start(f32[1,4,4,128]{3,1,2,0:T(4,128)S(1)} %copy.70) | copy-start | bytes 24580
  149.6 107.6 %all-to-all-start.2 = ((bf16[16,256,768]{2,1,0:T(8,128)(2,1)}), bf16[16,256,768]{2,1,0:T(8,128)(2,1)}, u32[]{:S(2)}, u32[]{:S(2)}) async-start(bf16[16,256,768]{2,1,0:T(8,128)(2,1)} %bitcast.104), calls=%async_computation.2 | async-start | bytes 12582912 | tf_op jit(solution)/shard_map/all_to_all | solution.py:397
  155.5 82.6 %copy-start.8 = (f32[768,10]{1,0:T(8,128)}, f32[768,10]{1,0:T(8,128)S(1)}, u32[]{:S(2)}) copy-start(f32[768,10]{1,0:T(8,128)S(1)} %reshape.253) | copy-start | bytes 92164
  243.0 14.2 %copy-start.34 = (f32[2048]{0:T(1024)}, f32[2048]{0:T(1024)S(1)}, u32[]{:S(2)}) copy-start(f32[2048]{0:T(1024)S(1)} %add_divide_fusion) | copy-start | bytes 24580
  257.2 81.7 %all-to-all-start.1 = ((bf16[16,256,768]{2,1,0:T(8,128)(2,1)}), bf16[16,256,768]{2,1,0:T(8,128)(2,1)}, u32[]{:S(2)}, u32[]{:S(2)}) async-start(bf16[16,256,768]{2,1,0:T(8,128)(2,1)} %bitcast.105), calls=%async_computation.1 | async-start | bytes 12582912 | tf_op jit(solution)/shard_map/all_to_all | solution.py:397
  261.1 744.3 %reduce-scatter.14.cloned.1.call-start = ((), (), s32[]{:S(2)}) async-start(), calls=%async_computation.23 | async-start | bytes 14155776 | tf_op jit(solution)/shard_map/reduce_scatter | solution.py:413
  440.5 569.6 %reduce-scatter.10.cloned.1.call-start = ((), (), s32[]{:S(2)}) async-start(), calls=%async_computation.21 | async-start | bytes 14155776 | tf_op jit(solution)/shard_map/reduce_scatter | solution.py:413
  468.9 642.9 %reduce-scatter.12.cloned.1.call-start = ((), (), s32[]{:S(2)}) async-start(), calls=%async_computation.22 | async-start | bytes 14155776 | tf_op jit(solution)/shard_map/reduce_scatter | solution.py:413
  545.4 82.2 %all-to-all-start.7 = ((bf16[16,256,768]{2,1,0:T(8,128)(2,1)}), bf16[16,256,768]{2,1,0:T(8,128)(2,1)}, u32[]{:S(2)}, u32[]{:S(2)}) async-start(bf16[16,256,768]{2,1,0:T(8,128)(2,1)} %bitcast.107), calls=%async_computation.7 | async-start | bytes 12582912 | tf_op jit(solution)/shard_map/all_to_all | solution.py:397
  550.3 716.9 %reduce-scatter.6.cloned.1.call-start = ((), (), s32[]{:S(2)}) async-start(), calls=%async_computation.19 | async-start | bytes 10027008 | tf_op jit(solution)/shard_map/reduce_scatter | solution.py:501
  550.4 77.2 %copy-start.25 = (s32[2048]{0:T(1024)}, s32[2048]{0:T(1024)S(1)}, u32[]{:S(2)}) copy-start(s32[2048]{0:T(1024)S(1)} %broadcast_clamp_fusion) | copy-start | bytes 24580
  684.1 27.1 %copy-start.9 = (f32[768,10]{1,0:T(8,128)S(1)}, f32[768,10]{1,0:T(8,128)}, u32[]{:S(2)}) copy-start(f32[768,10]{1,0:T(8,128)} %copy-done.8) | copy-start | bytes 92164
  684.1 27.1 %copy-start.18 = (s32[1,4,4,128]{3,1,2,0:T(4,128)S(1)}, s32[1,4,4,128]{3,1,2,0:T(4,128)}, u32[]{:S(2)}) copy-start(s32[1,4,4,128]{3,1,2,0:T(4,128)} %copy-done.17) | copy-start | bytes 24580
  842.3 429.8 %reduce-scatter.8.cloned.1.call-start = ((), (), s32[]{:S(2)}) async-start(), calls=%async_computation.20 | async-start | bytes 30081024 | tf_op jit(solution)/shard_map/reduce_scatter | solution.py:474
  911.5 85.0 %all-to-all-start.6 = ((bf16[16,256,768]{2,1,0:T(8,128)(2,1)}), bf16[16,256,768]{2,1,0:T(8,128)(2,1)}, u32[]{:S(2)}, u32[]{:S(2)}) async-start(bf16[16,256,768]{2,1,0:T(8,128)(2,1)} %bitcast.106), calls=%async_computation.6 | async-start | bytes 12582912 | tf_op jit(solution)/shard_map/all_to_all | solution.py:397
  1005.4 101.7 %all-to-all-start.11 = ((f32[8,192,768]{2,1,0:T(8,128)}), f32[8,192,768]{2,1,0:T(8,128)}, u32[]{:S(2)}, u32[]{:S(2)}) async-start(f32[8,192,768]{2,1,0:T(8,128)} %bitcast.110), calls=%async_computation.16 | async-start | bytes 9437184 | tf_op jit(solution)/shard_map/all_to_all | solution.py:397
  1107.2 83.3 %all-to-all-start.9 = ((f32[8,48,3072]{2,1,0:T(8,128)}), f32[8,48,3072]{2,1,0:T(8,128)}, u32[]{:S(2)}, u32[]{:S(2)}) async-start(f32[8,48,3072]{2,1,0:T(8,128)} %bitcast.109), calls=%async_computation.12 | async-start | bytes 9437184 | tf_op jit(solution)/shard_map/all_to_all | solution.py:397
  1190.5 69.9 %all-to-all-start.10 = ((f32[8,48,3072]{2,1,0:T(8,128)}), f32[8,48,3072]{2,1,0:T(8,128)}, u32[]{:S(2)}, u32[]{:S(2)}) async-start(f32[8,48,3072]{2,1,0:T(8,128)} %bitcast.108), calls=%async_computation.14 | async-start | bytes 9437184 | tf_op jit(solution)/shard_map/all_to_all | solution.py:397
  (25 other events, 179.6 us)
Sparse Core Ops, SparseCore 0:
  12.7 56.1 all-gather.8
  70.5 13.9 all-gather.12
  90.0 11.6 all-gather.14
  124.2 11.6 all-gather.16
  138.0 136.5 all-gather.10
  440.6 16.6 reduce-scatter.13
  469.0 16.6 reduce-scatter.9
  497.8 16.9 reduce-scatter.11
  842.4 102.8 reduce-scatter.5
  950.0 271.2 reduce-scatter.7
